TPU v7x, 128 devices: a whole 4x4x4 slice. The times are simulated.
128 devices in a mesh: fsdp: 64 (over x_lo, y, z, core), grp: 2 (over x_hi).
Axes of the slice: x: 4 (x_hi: 2, x_lo: 2; x = x_hi * 2 + x_lo), y: 4, z: 4, core: 2. Of those that a mesh axis runs over, the one named last changes fastest.
Arguments:
- hidden: bfloat16 [32768, 3072], P('fsdp', 'grp'), may hold values from -16 to 16
- queries: bfloat16 [32768, 1536], P('fsdp', 'grp'), may hold values from -6 to 6
- attn_keys: bfloat16 [32768, 1536], P('fsdp', 'grp'), may hold values from -6 to 6
- w_value: bfloat16 [1536, 3072], P('fsdp', 'grp'), may hold values from -1 to 1
- w_out: bfloat16 [1536, 3072], P('fsdp', 'grp'), may hold values from -1 to 1
- alpha: float32 [3072], P('grp'), may hold values from 0.05 to 0.5
- out_grad: bfloat16 [32768, 3072], P('fsdp', 'grp'), may hold values from -6 to 6
Outputs:
- new_hidden: bfloat16 [32768, 3072], P('fsdp', 'grp')
- grad_hidden: bfloat16 [32768, 3072], P('fsdp', 'grp')
- grad_queries: bfloat16 [32768, 1536], P('fsdp', 'grp')
- grad_keys: bfloat16 [32768, 1536], P('fsdp', 'grp')
- grad_w_value: float32 [1536, 3072], P('fsdp', 'grp')
- grad_w_out: float32 [1536, 3072], P('fsdp', 'grp')
All inputs are finite; a program needn't handle non-finite values.
Results may differ from a plain program's by a relative error of at most 0.012.
The roundings to bfloat16 on the way count: a program that leaves them out, or rounds other values in their place, can miss the bound.
Values may be sent and summed in bfloat16 or wider, within the bound.
No kernel may reach another device: no remote copies, remote signals or barrier semaphores. Data moves between devices by JAX's collectives and lax.ppermute only.
A program may use at most 192 MiB of HBM per device.

v0:
```python
import jax
import jax.numpy as jnp
from jax import lax
from jax.experimental import pallas as pl
from jax.experimental.pallas import tpu as pltpu
from jax.sharding import Mesh
from jax.sharding import PartitionSpec as P


D = 3072
HS = 128
X, Y, Z, C, G = "fsdp_0", "fsdp_1", "fsdp_2", "fsdp_3", "grp"
FSDP = (X, Y, Z, C)
YZ = (Y, Z)
EPS = 1e-06
SWAP = [(0, 1), (1, 0)]
ACROSS = [(0, 3), (1, 2), (2, 1), (3, 0)]
F32 = jnp.float32
BF16 = jnp.bfloat16


def contract_last(left, right):
    return lax.dot_general(left, right, (((1,), (1,)), ((), ())), preferred_element_type=F32)


def contract_first(left, right):
    return lax.dot_general(left, right, (((0,), (0,)), ((), ())), preferred_element_type=F32)


def matmul(left, right):
    return jnp.dot(left, right, preferred_element_type=F32)


def probs_kernel(q_ref, k_ref, p_ref):
    length = q_ref.shape[0]
    scores = contract_last(q_ref[...], k_ref[...]) * (HS**-0.5)
    row_pos = lax.broadcasted_iota(jnp.int32, (length, length), 0)
    col_pos = lax.broadcasted_iota(jnp.int32, (length, length), 1)
    scores = jnp.where(row_pos >= col_pos, scores, -1e30)
    terms = jnp.exp(scores - jnp.max(scores, axis=1, keepdims=True))
    p_ref[0] = terms * (1.0 / jnp.sum(terms, axis=1, keepdims=True))


def forward_kernel(p_ref, own_ref, peer_ref, rate_ref, v_ref, attn_ref):
    value = ((own_ref[...] + peer_ref[...].astype(F32)) * rate_ref[0:1, :]).astype(BF16)
    v_ref[...] = value
    attn_ref[...] = matmul(p_ref[0].astype(BF16), value).astype(BF16)


def backward_kernel(q_ref, k_ref, v_ref, p_ref, own_ref, peer_ref, dq_ref, dk_ref, dv_ref):
    scale = HS**-0.5
    prob = p_ref[0]
    grad = (own_ref[...] + peer_ref[...].astype(F32)).astype(BF16)
    grad_prob = contract_last(grad, v_ref[...])
    delta = jnp.sum(prob * grad_prob, axis=1, keepdims=True)
    grad_score = (prob * (grad_prob - delta)).astype(BF16)
    dv_ref[...] = contract_first(prob.astype(BF16), grad).astype(BF16)
    dq_ref[...] = (matmul(grad_score, k_ref[...]) * scale).astype(BF16)
    dk_ref[...] = (contract_first(grad_score, q_ref[...]) * scale).astype(BF16)


def heads_call(kernel, heads, operands, results, dots):
    def spec(shape, first):
        if len(shape) == 3:
            return pl.BlockSpec((1, *shape[1:]), lambda h: (first + h, 0, 0))
        return pl.BlockSpec((shape[0], HS), lambda h: (0, first + h))

    tokens = operands[0][0].shape[-2]
    return pl.pallas_call(
        kernel,
        grid=(heads,),
        in_specs=[spec(o.shape, first) for o, first in operands],
        out_specs=[spec(shape, first) for shape, _, first in results],
        out_shape=[jax.ShapeDtypeStruct(shape, dtype) for shape, dtype, _ in results],
        cost_estimate=pl.CostEstimate(
            flops=4 * dots * heads * tokens * tokens * HS,
            bytes_accessed=heads * tokens * (tokens * 4 + HS * 10),
            transcendentals=0,
        ),
        compiler_params=pltpu.CompilerParams(dimension_semantics=("arbitrary",)),
    )(*[o for o, _ in operands])


def exchanged(value, axis=G):
    return lax.ppermute(value, axis, SWAP)


def chosen(first_if, first, second):
    return jnp.where(first_if, first, second)


def columns(value, index):
    half = value.shape[-1] // 2
    return jnp.where(index == 0, value[..., :half], value[..., half:])


def in_order(index, mine, other, axis):
    return jnp.where(
        index == 0,
        jnp.concatenate([mine, other], axis),
        jnp.concatenate([other, mine], axis),
    )


def over_planes(rows):
    planes = lax.axis_size(Y) * lax.axis_size(Z)
    got = lax.all_to_all(jnp.broadcast_to(rows[None], (planes, *rows.shape)), YZ, 0, 0, tiled=True)
    return got.swapaxes(0, 1) if rows.ndim == 3 else got.reshape(-1, rows.shape[-1])


def product_kernel(*refs):
    *lefts, near_ref, other_ref, out_ref = refs
    runs, _, each, width = out_ref.shape
    for i in range(len(lefts) // 2):
        total = contract_first(lefts[2 * i][...], near_ref[...])
        total = total + contract_first(lefts[2 * i + 1][...], other_ref[...])
        out_ref[:, i] = total.astype(BF16).reshape(runs, each, width)


def products(lefts, near, other, each, steps=2):
    tokens, count = lefts[0].shape
    width = near.shape[1]
    block = count // steps
    pairs = len(lefts) // 2
    return pl.pallas_call(
        product_kernel,
        grid=(steps,),
        in_specs=[pl.BlockSpec((tokens, block), lambda i: (0, i))] * len(lefts)
        + [pl.BlockSpec((tokens, width), lambda i: (0, 0))] * 2,
        out_specs=pl.BlockSpec((block // each, pairs, each, width), lambda i: (i, 0, 0, 0)),
        out_shape=jax.ShapeDtypeStruct((count // each, pairs, each, width), BF16),
        cost_estimate=pl.CostEstimate(
            flops=2 * tokens * count * width * len(lefts),
            bytes_accessed=4 * count * width,
            transcendentals=0,
        ),
        compiler_params=pltpu.CompilerParams(dimension_semantics=("arbitrary",)),
    )(*lefts, near, other)


def arriving(tiles, after=None):
    if after is not None:
        tiles, _ = lax.optimization_barrier((tiles, after))
    return lax.all_to_all(tiles, YZ, 0, 0, tiled=True)


def summed(arrived):
    return jnp.sum(arrived.astype(F32), axis=0)


def owned(own, peer, at_own, core, unit):
    keep, send = chosen(at_own, own, peer), chosen(at_own, peer, own)
    count = keep.shape[0] // 2

    def part(value, index):
        return chosen(index == 0, value[:count], value[count:])

    far = lax.ppermute(part(send, 1 - core), (X, C), ACROSS)
    near = part(keep, core) + exchanged(part(send, core), X)
    far = far + exchanged(part(keep, 1 - core), C)
    rows = in_order(core, near, far, 1)
    dots = jnp.sum(rows * unit, axis=1)
    return rows, (dots + exchanged(dots))[:, None]


def shards(hidden, queries, attn_keys, w_value, w_out, alpha, out_grad):
    rows = w_value.shape[0]
    tokens, width = queries.shape
    heads = width // HS
    side, core, grp = lax.axis_index(X), lax.axis_index(C), lax.axis_index(G)
    at_own = side == grp

    next_v = exchanged(w_value, X)
    pair_v = jnp.stack((chosen(at_own, next_v, w_value), chosen(at_own, w_value, next_v)))
    other_v = exchanged(columns(pair_v, 1 - core), C)
    pair_v = in_order(core, columns(pair_v, core), other_v, 1)
    raw_near = over_planes(pair_v)
    raw_far = exchanged(raw_near, C)
    raw_near, raw_far = (w.reshape(2, width, -1) for w in (raw_near, raw_far))

    next_o = exchanged(w_out, X)
    own_vf, own_of = w_value.astype(F32), w_out.astype(F32)
    next_of = next_o.astype(F32)
    own_part = jnp.stack((jnp.sum(own_of * own_of, axis=1), jnp.sum(own_vf * own_vf, axis=1)))
    next_part = jnp.sum(next_of * next_of, axis=1)
    own_sq = own_part + lax.ppermute(own_part, G, SWAP)
    next_sq = next_part + lax.ppermute(own_part[0], (X, G), ACROSS)
    norm_o, norm_v = jnp.sqrt(own_sq[0] + EPS)[:, None], jnp.sqrt(own_sq[1] + EPS)[:, None]
    unit_v, unit_o = own_vf / norm_v, own_of / norm_o
    here = unit_o.astype(BF16)
    there = (next_of / jnp.sqrt(next_sq + EPS)[:, None]).astype(BF16)
    pair_o = jnp.stack((chosen(at_own, here, there), chosen(at_own, there, here)))
    send_o = columns(pair_o, 1 - core)
    other_o = exchanged(send_o, C)
    pair_o = in_order(core, columns(pair_o, core), other_o, 1)
    pair_o, _ = lax.optimization_barrier((pair_o, raw_near))
    both_o = over_planes(pair_o)
    both_o_far = exchanged(both_o, C)
    weight_o = in_order(core, both_o, both_o_far, 3)
    weight_o = weight_o.reshape(2, width, -1)
    weight_o_own, weight_o_peer = weight_o[0], weight_o[1]

    (probs,) = heads_call(
        probs_kernel, heads, ((queries, 0), (attn_keys, 0)), (((heads, tokens, tokens), F32, 0),), 1
    )
    hidden_near, hidden_far = lax.optimization_barrier(
        (columns(hidden, core), columns(hidden, 1 - core))
    )
    hidden_other = exchanged(hidden_far, C)
    full = (tokens, width)
    part = contract_last(hidden_near, raw_near[0]) + contract_last(hidden_far, raw_far[0])
    part = part.astype(BF16)
    value_peer = exchanged(part)
    value_own = contract_last(hidden_near, raw_near[1]) + contract_last(hidden_far, raw_far[1])
    near, far, _ = lax.optimization_barrier((raw_near, raw_far, part))
    half_sq = jnp.sum(jnp.square(near.astype(F32)), axis=2)
    half_sq = half_sq + jnp.sum(jnp.square(far.astype(F32)), axis=2)
    all_sq = half_sq + exchanged(half_sq)[::-1]
    own_rate = jnp.broadcast_to(lax.rsqrt(all_sq[1] + EPS)[None], (8, width))
    values, attn_own = heads_call(
        forward_kernel,
        heads,
        ((probs, 0), (value_own, 0), (value_peer, 0), (own_rate, 0)),
        ((full, BF16, 0), (full, BF16, 0)),
        1,
    )
    attn_their = exchanged(attn_own)
    weight_v = in_order(core, near, far, 2).astype(F32) / jnp.sqrt(all_sq + EPS)[..., None]
    weight_v_peer, weight_v_own = weight_v[0].astype(BF16), weight_v[1].astype(BF16)

    attn_own_other = exchanged(attn_own, C)
    proj = lax.optimization_barrier(matmul(attn_own, weight_o_own))
    attn_their_other = exchanged(attn_their, C)
    proj = proj + matmul(attn_their, weight_o_peer)
    hidden_f = hidden.astype(F32)
    grad_out = out_grad.astype(F32)
    keep_rate = 1.0 - alpha
    moments = jnp.stack(
        (
            jnp.sum(proj * proj, axis=1),
            jnp.sum(keep_rate * keep_rate * hidden_f * hidden_f, axis=1),
            jnp.sum(keep_rate * alpha * hidden_f * proj, axis=1),
            jnp.sum(alpha * alpha * proj * proj, axis=1),
            jnp.sum(grad_out * keep_rate * hidden_f, axis=1),
            jnp.sum(grad_out * alpha * proj, axis=1),
        )
    )
    moments = moments + exchanged(moments)
    proj_rs = lax.rsqrt(moments[0] / D + EPS)[:, None]
    cross_sum = moments[2][:, None]
    alpha_sum = moments[3][:, None]
    mix_mean = (moments[1][:, None] + 2.0 * proj_rs * cross_sum + proj_rs * proj_rs * alpha_sum) / D
    mix_rs = lax.rsqrt(mix_mean + EPS)
    mixed = hidden_f + alpha * (proj * proj_rs - hidden_f)
    new_hidden = (mixed * mix_rs).astype(BF16)
    grad_mean = (moments[4][:, None] + proj_rs * moments[5][:, None]) / D
    grad_mix = mix_rs * (grad_out - mixed * mix_rs * mix_rs * grad_mean)
    grad_pn = grad_mix * alpha
    proj_mean = (
        mix_rs * moments[5][:, None]
        - mix_rs * mix_rs * mix_rs * grad_mean * (cross_sum + proj_rs * alpha_sum)
    ) / D
    grad_res = grad_mix * keep_rate
    grad_proj = proj_rs * (grad_pn - proj * proj_rs * proj_rs * proj_mean)
    grad_proj_b = grad_proj.astype(BF16)

    grad_near, grad_far = lax.optimization_barrier(
        (columns(grad_proj_b, core), columns(grad_proj_b, 1 - core))
    )
    grad_other = exchanged(grad_far, C)
    part = contract_last(grad_proj_b, weight_o_peer).astype(BF16)
    grad_peer = exchanged(part)
    grad_own = contract_last(grad_proj_b, weight_o_own)
    lefts = (attn_own, attn_own_other, attn_their, attn_their_other)
    at_o = arriving(products(lefts, grad_near, grad_other, 2 * rows))
    gw_o = summed(at_o)
    grad_q, grad_k, gv_own = heads_call(
        backward_kernel,
        heads,
        tuple((o, 0) for o in (queries, attn_keys, values, probs, grad_own, grad_peer)),
        ((full, BF16, 0),) * 3,
        4,
    )
    gv_peer = exchanged(gv_own)

    gv_own_other = exchanged(gv_own, C)
    tiles = products((gv_own, gv_own_other), hidden_near, hidden_other, 2 * rows)
    at_own_v = arriving(tiles, at_o)
    gw_v_own = summed(at_own_v)[0]
    gv_peer_other = exchanged(gv_peer, C)
    tiles = products((gv_peer, gv_peer_other), hidden_near, hidden_other, 2 * rows)
    gw_v_peer = summed(arriving(tiles, at_own_v))[0]
    from_own = lax.optimization_barrier(matmul(gv_own, weight_v_own))
    from_peer = matmul(gv_peer, weight_v_peer)
    grad_hidden = (grad_res + from_own + from_peer).astype(BF16)
    gw_o_mine, dot_o = owned(gw_o[0], gw_o[1], at_own, core, unit_o)
    gw_v_mine, dot_v = owned(gw_v_own, gw_v_peer, at_own, core, unit_v)
    grad_w_value = (gw_v_mine - unit_v * dot_v) / norm_v
    grad_w_out = (gw_o_mine - unit_o * dot_o) / norm_o
    return new_hidden, grad_hidden, grad_q, grad_k, grad_w_value, grad_w_out


def solution(mesh):
    torus = Mesh(mesh.devices.reshape(2, 4, 4, 2, mesh.shape[G]), (*FSDP, G))
    placed = P(FSDP, G)
    return jax.shard_map(
        shards,
        mesh=torus,
        in_specs=(placed,) * 5 + (P(G), placed),
        out_specs=(placed,) * 6,
        check_vma=False,
    )
```

profile of v0, /device:TPU:6, one launch (start us, length us, event | category | flops | bytes accessed | tf_op | source)
XLA Modules:
  0.0 308.8 jit_solution(3570424776987789477)
XLA Ops:
  1.5 3.7 %collective-permute-done = bf16[24,1536]{1,0:T(8,128)(2,1)S(1)} collective-permute-done((bf16[24,1536]{1,0:T(8,128)(2,1)}, bf16[24,1536]{1,0:T(8,128)(2,1)S(1)}, u32[]{:S(2)}, u32[]{:S(2)}) %collective-permute-start) | collective-permute-done | bytes 73760 | tf_op jit(solution)/shard_map/ppermute | solution.py:85
  7.6 1.7 broadcast_in_dim.8
  9.3 8.1 %all-to-all-start = ((bf16[16,2,48,768]{3,2,1,0:T(8,128)(2,1)}), bf16[16,2,48,768]{3,2,1,0:T(8,128)(2,1)}, u32[]{:S(2)}, u32[]{:S(2)}) async-start(bf16[16,2,48,768]{3,2,1,0:T(8,128)(2,1)} %broadcast_in_dim.8), calls=%async_computation | async-start | bytes 4718592 | tf_op jit(solution)/shard_map/all_to_all | solution.py:107
  17.7 1.5 collective-permute-start.5
  19.1 2.7 collective-permute-start.7
  25.5 25.6 %all-to-all-done = bf16[16,2,48,768]{3,2,1,0:T(8,128)(2,1)} async-done(((bf16[16,2,48,768]{3,2,1,0:T(8,128)(2,1)}), bf16[16,2,48,768]{3,2,1,0:T(8,128)(2,1)}, u32[]{:S(2)}, u32[]{:S(2)}) %all-to-all-start) | async-done | bytes 2359328 | tf_op jit(solution)/shard_map/all_to_all | solution.py:107
  51.1 1.8 copy.16
  52.9 1.7 broadcast_in_dim.11
  54.6 5.2 %all-to-all-start.1 = ((bf16[16,2,48,768]{3,2,1,0:T(8,128)(2,1)}), bf16[16,2,48,768]{3,2,1,0:T(8,128)(2,1)}, u32[]{:S(2)}, u32[]{:S(2)}) async-start(bf16[16,2,48,768]{3,2,1,0:T(8,128)(2,1)} %broadcast_in_dim.11), calls=%async_computation.1 | async-start | bytes 4718592 | tf_op jit(solution)/shard_map/all_to_all | solution.py:107
  59.9 2.4 broadcast_select_fusion.1
  62.3 6.9 %shard_map.118.p_ref = f32[6,512,512]{2,1,0:T(8,128)} custom-call(bf16[512,768]{1,0:T(8,128)(2,1)} %q_ref.3, bf16[512,768]{1,0:T(8,128)(2,1)} %k_ref.3), custom_call_target="tpu_custom_call" | custom-call | flops 805306368 | bytes 10223616 | tf_op jit(solution)/shard_map/pallas_call | solution.py:69
  69.2 1.6 fusion.33
  70.7 21.3 %all-to-all-done.1 = bf16[16,2,48,768]{3,2,1,0:T(8,128)(2,1)} async-done(((bf16[16,2,48,768]{3,2,1,0:T(8,128)(2,1)}), bf16[16,2,48,768]{3,2,1,0:T(8,128)(2,1)}, u32[]{:S(2)}, u32[]{:S(2)}) %all-to-all-start.1) | async-done | bytes 2359328 | tf_op jit(solution)/shard_map/all_to_all | solution.py:107
  92.0 2.5 fusion.35
  95.3 1.8 fusion.32
  97.1 1.7 add_convert_fusion.1
  100.2 2.7 multiply_reduce_fusion
  102.9 2.2 collective-permute-start.4
  105.1 2.0 convolution_add_fusion.own_ref
  107.1 13.4 %collective-permute-done.4 = f32[2,768]{1,0:T(2,128)S(1)} collective-permute-done((f32[2,768]{1,0:T(2,128)S(1)}, f32[2,768]{1,0:T(2,128)S(1)}, u32[]{:S(2)}, u32[]{:S(2)}) %collective-permute-start.4) | collective-permute-done | bytes 6176 | tf_op jit(solution)/shard_map/ppermute | solution.py:85
  121.9 6.5 %shard_map.119 = (bf16[512,768]{1,0:T(8,128)(2,1)}, bf16[512,768]{1,0:T(8,128)(2,1)}) custom-call(f32[6,512,512]{2,1,0:T(8,128)} %shard_map.118.p_ref, f32[512,768]{1,0:T(8,128)} %convolution_add_fusion.own_ref, bf16[512,768]{1,0:T(8,128)(2,1)} %collective-permute-done.3.peer_ref, f32[8,768]{1,0:T(8,128)} %broadcast_in_dim.10.rate_ref), custom_call_target="tpu_custom_call" | custom-call | flops 805306368 | bytes 10223616 | tf_op jit(solution)/shard_map/pallas_call | solution.py:69
  129.8 5.0 %maximum_select_fusion = bf16[2,16,48,1536]{3,2,0,1:T(8,128)(2,1)S(1)} fusion(bf16[2,16,48,768]{3,2,0,1:T(8,128)(2,1)} %collective-permute-done.9, bf16[2,16,48,768]{3,2,0,1:T(8,128)(2,1)} %bitcast.15, pred[]{:T(512)S(6)} %eq.6), kind=kLoop, calls=%fused_computation.11 | loop fusion | flops 21233664 | bytes 9437185 | tf_op jit(solution)/shard_map/jit(_where)/select_n | solution.py:98
  137.4 11.8 %collective-permute-done.10.refs_2_ = bf16[512,768]{1,0:T(8,128)(2,1)S(1)} collective-permute-done((bf16[512,768]{1,0:T(8,128)(2,1)}, bf16[512,768]{1,0:T(8,128)(2,1)S(1)}, u32[]{:S(2)}, u32[]{:S(2)}) %collective-permute-start.10) | collective-permute-done | bytes 786464 | tf_op jit(solution)/shard_map/ppermute | solution.py:85
  151.3 3.8 %fusion.2 = (f32[512]{0:T(512)S(1)}, f32[512]{0:T(512)S(1)}, f32[512]{0:T(512)S(1)}, f32[512]{0:T(512)S(1)}, f32[512]{0:T(512)S(1)}, /*index=5*/f32[512]{0:T(512)S(1)}, f32[512,1536]{1,0:T(8,128)}) fusion(bf16[512,1536]{1,0:T(8,128)(2,1)S(1)} %copy-done.4, f32[1536]{0:T(1024)S(1)} %copy-done.17, f32[1536]{0:T(1024)S(1)} %get-tuple-element.82, ...), kind=kLoop, calls=%fused_computation.18 | loop fusion | flops 15725568 | bytes 12625920 | tf_op jit(solution)/shard_map/reduce_sum | solution.py:245
  157.1 3.3 %collective-permute-done.11 = f32[6,512]{1,0:T(8,128)S(1)} collective-permute-done((f32[6,512]{1,0:T(8,128)S(1)}, f32[6,512]{1,0:T(8,128)S(1)}, u32[]{:S(2)}, u32[]{:S(2)}) %collective-permute-start.11) | collective-permute-done | bytes 12320 | tf_op jit(solution)/shard_map/ppermute | solution.py:85
  160.5 4.8 %multiply_convert_fusion = (bf16[512,1536]{1,0:T(8,128)(2,1)S(1)}, bf16[512,1536]{1,0:T(8,128)(2,1)}) fusion(f32[512,1536]{1,0:T(8,128)} %get-tuple-element.42, bf16[512,1536]{1,0:T(8,128)(2,1)} %param.13, f32[512]{0:T(512)S(1)} %get-tuple-element.83, f32[512]{0:T(512)S(1)} %get-tuple-element.87, f32[512]{0:T(512)S(1)} %get-tuple-element.84, ...), kind=kLoop, calls=%fused_computation.27 | loop fusion | flops 14155776 | bytes 9451520 | tf_op jit(solution)/shard_map/convert_element_type | solution.py:265
  167.5 2.4 collective-permute-done.18.refs_5_
  169.9 5.9 %shard_map.122 = bf16[16,2,48,768]{3,2,1,0:T(8,128)(2,1)} custom-call(bf16[512,768]{1,0:T(8,128)(2,1)} %get-tuple-element.24.refs_0_, bf16[512,768]{1,0:T(8,128)(2,1)} %collective-permute-done.16.refs_1_, bf16[512,768]{1,0:T(8,128)(2,1)} %copy-done.28, bf16[512,768]{1,0:T(8,128)(2,1)} %collective-permute-done.17.refs_3_, ...), custom_call_target="tpu_custom_call" | custom-call | flops 2415919104 | bytes 2359296 | tf_op jit(solution)/shard_map/pallas_call | solution.py:125
  175.8 4.4 %all-to-all-start.2 = ((bf16[16,2,48,768]{3,2,1,0:T(8,128)(2,1)}), bf16[16,2,48,768]{3,2,1,0:T(8,128)(2,1)}, u32[]{:S(2)}, u32[]{:S(2)}) async-start(bf16[16,2,48,768]{3,2,1,0:T(8,128)(2,1)} %shard_map.122), calls=%async_computation.2 | async-start | bytes 4718592 | tf_op jit(solution)/shard_map/all_to_all | solution.py:144
  180.2 3.7 %convolution_convert_fusion = bf16[512,768]{1,0:T(8,128)(2,1)S(1)} fusion(bf16[512,1536]{1,0:T(8,128)(2,1)} %copy-done.2, bf16[768,1536]{1,0:T(8,128)(2,1)} %bitcast.80), kind=kOutput, calls=%fused_computation.37 | convolution fusion | flops 1208352768 | bytes 4718592 | tf_op jit(solution)/shard_map/dot_general | solution.py:23
  183.9 1.5 collective-permute-start.12
  185.4 2.6 fusion.39.own_ref
  188.0 17.2 %collective-permute-done.12.peer_ref = bf16[512,768]{1,0:T(8,128)(2,1)} collective-permute-done((bf16[512,768]{1,0:T(8,128)(2,1)S(1)}, bf16[512,768]{1,0:T(8,128)(2,1)}, u32[]{:S(2)}, u32[]{:S(2)}) %collective-permute-start.12) | collective-permute-done | bytes 786464 | tf_op jit(solution)/shard_map/ppermute | solution.py:85
  205.2 9.2 %shard_map.120 = (bf16[512,768]{1,0:T(8,128)(2,1)}, bf16[512,768]{1,0:T(8,128)(2,1)}, bf16[512,768]{1,0:T(8,128)(2,1)}) custom-call(bf16[512,768]{1,0:T(8,128)(2,1)} %q_ref.3, bf16[512,768]{1,0:T(8,128)(2,1)} %k_ref.3, bf16[512,768]{1,0:T(8,128)(2,1)} %get-tuple-element.26.v_ref, f32[6,512,512]{2,1,0:T(8,128)} %shard_map.118.p_ref, ...), custom_call_target="tpu_custom_call" | custom-call | flops 3221225472 | bytes 10223616 | tf_op jit(solution)/shard_map/pallas_call | solution.py:69
  216.4 18.6 %collective-permute-done.13.refs_0_ = bf16[512,768]{1,0:T(8,128)(2,1)} collective-permute-done((bf16[512,768]{1,0:T(8,128)(2,1)}, bf16[512,768]{1,0:T(8,128)(2,1)}, u32[]{:S(2)}, u32[]{:S(2)}) %collective-permute-start.13) | collective-permute-done | bytes 786464 | tf_op jit(solution)/shard_map/ppermute | solution.py:85
  235.9 4.1 %shard_map.121 = bf16[16,1,48,768]{3,2,1,0:T(8,128)(2,1)} custom-call(bf16[512,768]{1,0:T(8,128)(2,1)} %get-tuple-element.27.refs_0_, bf16[512,768]{1,0:T(8,128)(2,1)} %collective-permute-done.14.refs_1_, bf16[512,768]{1,0:T(8,128)(2,1)} %get-tuple-element.20.refs_2_, bf16[512,768]{1,0:T(8,128)(2,1)} %copy-done.30), custom_call_target="tpu_custom_call" | custom-call | flops 1207959552 | bytes 2359296 | tf_op jit(solution)/shard_map/pallas_call | solution.py:125
  240.0 6.8 %all-to-all-start.3 = ((bf16[16,1,48,768]{3,2,1,0:T(8,128)(2,1)}), bf16[16,1,48,768]{3,2,1,0:T(8,128)(2,1)S(1)}, u32[]{:S(2)}, u32[]{:S(2)}) async-start(bf16[16,1,48,768]{3,2,1,0:T(8,128)(2,1)} %shard_map.121), calls=%async_computation.3 | async-start | bytes 2359296 | tf_op jit(solution)/shard_map/all_to_all | solution.py:144
  246.8 6.2 %divide_convert_fusion = bf16[2,768,1536]{2,1,0:T(8,128)(2,1)} fusion(bf16[2,768,768]{2,1,0:T(8,128)(2,1)} %bitcast.8, bf16[2,768,768]{2,1,0:T(8,128)(2,1)S(1)} %bitcast.75, f32[2,768]{1,0:T(2,128)} %get-tuple-element.40, pred[]{:T(512)S(6)} %eq.6), kind=kLoop, calls=%fused_computation | loop fusion | flops 28311552 | bytes 9443329 | tf_op jit(solution)/shard_map/convert.1
  253.0 4.1 %shard_map.123 = bf16[16,1,48,768]{3,2,1,0:T(8,128)(2,1)} custom-call(bf16[512,768]{1,0:T(8,128)(2,1)} %collective-permute-done.13.refs_0_, bf16[512,768]{1,0:T(8,128)(2,1)} %collective-permute-done.19.refs_1_, bf16[512,768]{1,0:T(8,128)(2,1)} %get-tuple-element.20.refs_2_, bf16[512,768]{1,0:T(8,128)(2,1)} %copy-done.30), custom_call_target="tpu_custom_call" | custom-call | flops 1207959552 | bytes 2359296 | tf_op jit(solution)/shard_map/pallas_call | solution.py:125
  257.1 2.1 convert_reduce_fusion
  259.2 7.6 %all-to-all-done.3 = bf16[16,1,48,768]{3,2,1,0:T(8,128)(2,1)S(1)} async-done(((bf16[16,1,48,768]{3,2,1,0:T(8,128)(2,1)}), bf16[16,1,48,768]{3,2,1,0:T(8,128)(2,1)S(1)}, u32[]{:S(2)}, u32[]{:S(2)}) %all-to-all-start.3) | async-done | bytes 1179680 | tf_op jit(solution)/shard_map/all_to_all | solution.py:144
  266.8 4.4 %all-to-all-start.4 = ((bf16[16,1,48,768]{3,2,1,0:T(8,128)(2,1)}), bf16[16,1,48,768]{3,2,1,0:T(8,128)(2,1)}, u32[]{:S(2)}, u32[]{:S(2)}) async-start(bf16[16,1,48,768]{3,2,1,0:T(8,128)(2,1)} %shard_map.123), calls=%async_computation.4 | async-start | bytes 2359296 | tf_op jit(solution)/shard_map/all_to_all | solution.py:144
  273.5 4.8 %fusion.11 = f32[512,1536]{1,0:T(8,128)} fusion(bf16[512,768]{1,0:T(8,128)(2,1)S(1)} %copy-done.29, bf16[2,768,1536]{2,1,0:T(8,128)(2,1)} %divide_convert_fusion), kind=kOutput, calls=%fused_computation.32 | convolution fusion | flops 1207959552 | bytes 6291456 | tf_op jit(solution)/shard_map/dot_general | solution.py:31
  280.9 8.5 %all-to-all-done.4 = bf16[16,1,48,768]{3,2,1,0:T(8,128)(2,1)} async-done(((bf16[16,1,48,768]{3,2,1,0:T(8,128)(2,1)}), bf16[16,1,48,768]{3,2,1,0:T(8,128)(2,1)}, u32[]{:S(2)}, u32[]{:S(2)}) %all-to-all-start.4) | async-done | bytes 1179680 | tf_op jit(solution)/shard_map/all_to_all | solution.py:144
  293.2 2.2 collective-permute-done.20
  295.5 7.1 %add_convert_fusion = bf16[512,1536]{1,0:T(8,128)(2,1)} fusion(f32[512,1536]{1,0:T(8,128)} %fusion.11, bf16[512,768]{1,0:T(8,128)(2,1)} %collective-permute-done.13.refs_0_, bf16[2,768,1536]{2,1,0:T(8,128)(2,1)} %divide_convert_fusion, bf16[512,1536]{1,0:T(8,128)(2,1)S(1)} %copy-done.5, f32[512]{0:T(512)S(1)} %copy-done.25, f32[512]{0:T(512)S(1)} %copy-done.23, ...), kind=kOutput, calls=%fused_computation.26 | convolution fusion | flops 1219756032 | bytes 14174208 | tf_op jit(solution)/shard_map/dot_general | solution.py:31
  302.9 2.2 collective-permute-start.23
  305.9 2.1 collective-permute-done.23
  (150 shorter events, 34.5 us)
Async XLA Ops:
  0.6 4.6 %collective-permute-start = (bf16[24,1536]{1,0:T(8,128)(2,1)}, bf16[24,1536]{1,0:T(8,128)(2,1)S(1)}, u32[]{:S(2)}, u32[]{:S(2)}) collective-permute-start(bf16[24,1536]{1,0:T(8,128)(2,1)} %param.10), channel_id=1, source_target_pairs={{0,64},{64,0},{1,65},{65,1},{2,66},{66,2},{3,67},{67,3},{4,68},{68... | collective-permute-start | bytes 221192 | tf_op jit(solution)/shard_map/ppermute | solution.py:85
  6.2 1.3 collective-permute-start.1
  7.6 9.8 %copy-start.13 = (bf16[24,1536]{1,0:T(8,128)(2,1)S(1)}, bf16[24,1536]{1,0:T(8,128)(2,1)}, u32[]{:S(2)}) copy-start(bf16[24,1536]{1,0:T(8,128)(2,1)} %param.10) | copy-start | bytes 221188
  7.6 9.9 %copy-start.11 = (bf16[24,1536]{1,0:T(8,128)(2,1)S(1)}, bf16[24,1536]{1,0:T(8,128)(2,1)}, u32[]{:S(2)}) copy-start(bf16[24,1536]{1,0:T(8,128)(2,1)} %param.11) | copy-start | bytes 221188
  9.3 41.8 %all-to-all-start = ((bf16[16,2,48,768]{3,2,1,0:T(8,128)(2,1)}), bf16[16,2,48,768]{3,2,1,0:T(8,128)(2,1)}, u32[]{:S(2)}, u32[]{:S(2)}) async-start(bf16[16,2,48,768]{3,2,1,0:T(8,128)(2,1)} %broadcast_in_dim.8), calls=%async_computation | async-start | bytes 4718592 | tf_op jit(solution)/shard_map/all_to_all | solution.py:107
  17.7 5.2 %collective-permute-start.5 = (f32[2,24]{1,0:T(2,128)S(1)}, f32[2,24]{1,0:T(2,128)S(1)}, u32[]{:S(2)}, u32[]{:S(2)}) collective-permute-start(f32[2,24]{1,0:T(2,128)S(1)} %pad_maximum_fusion.2), channel_id=1, source_target_pairs={{0,1},{1,0},{2,3},{3,2},{4,5},{5,4},{6,7},{7,6},{8,9},{9,8},{10,11... | collective-permute-start | bytes 584 | tf_op jit(solution)/shard_map/ppermute | solution.py:186
  19.1 4.4 %collective-permute-start.6 = (bf16[24,1536]{1,0:T(8,128)(2,1)S(1)}, bf16[24,1536]{1,0:T(8,128)(2,1)S(1)}, u32[]{:S(2)}, u32[]{:S(2)}) collective-permute-start(bf16[24,1536]{1,0:T(8,128)(2,1)S(1)} %copy-done.11), channel_id=1, source_target_pairs={{0,64},{64,0},{1,65},{65,1},{2,66},{66,2},{3,67},{67,3},{4,68},{68... | collective-permute-start | bytes 221192 | tf_op jit(solution)/shard_map/ppermute | solution.py:85
  19.1 4.8 %collective-permute-start.7 = (f32[24]{0:T(128)S(1)}, f32[24]{0:T(128)S(1)}, u32[]{:S(2)}, u32[]{:S(2)}) collective-permute-start(f32[24]{0:T(128)S(1)} %fusion.12), channel_id=1, source_target_pairs={{0,65},{1,64},{64,1},{65,0},{2,67},{3,66},{66,3},{67,2},{4,69},{5,... | collective-permute-start | bytes 296 | tf_op jit(solution)/shard_map/ppermute | solution.py:187
  24.1 1.3 collective-permute-start.8
  54.6 37.4 %all-to-all-start.1 = ((bf16[16,2,48,768]{3,2,1,0:T(8,128)(2,1)}), bf16[16,2,48,768]{3,2,1,0:T(8,128)(2,1)}, u32[]{:S(2)}, u32[]{:S(2)}) async-start(bf16[16,2,48,768]{3,2,1,0:T(8,128)(2,1)} %broadcast_in_dim.11), calls=%async_computation.1 | async-start | bytes 4718592 | tf_op jit(solution)/shard_map/all_to_all | solution.py:107
  59.8 35.5 %collective-permute-start.2 = (bf16[2,16,48,768]{3,2,1,0:T(8,128)(2,1)S(1)}, bf16[2,16,48,768]{3,2,1,0:T(8,128)(2,1)}, u32[]{:S(2)}, u32[]{:S(2)}) collective-permute-start(bf16[2,16,48,768]{3,2,1,0:T(8,128)(2,1)S(1)} %bitcast.72), channel_id=1, source_target_pairs={{0,2},{2,0},{1,3},{3,1},{4,6},{6,4},{5,7},{7,5},{8,10},{10,8},{9,1... | collective-permute-start | bytes 7077896 | tf_op jit(solution)/shard_map/ppermute | solution.py:85
  62.3 6.9 %copy-start.17 = (f32[1536]{0:T(1024)S(1)}, f32[1536]{0:T(1024)}, u32[]{:S(2)}) copy-start(f32[1536]{0:T(1024)} %param.12) | copy-start | bytes 18436
  92.0 37.8 %collective-permute-start.9 = (bf16[2,16,48,768]{3,2,0,1:T(8,128)(2,1)}, bf16[2,16,48,768]{3,2,0,1:T(8,128)(2,1)}, u32[]{:S(2)}, u32[]{:S(2)}) collective-permute-start(bf16[2,16,48,768]{3,2,0,1:T(8,128)(2,1)} %bitcast.15), channel_id=1, source_target_pairs={{0,2},{2,0},{1,3},{3,1},{4,6},{6,4},{5,7},{7,5},{8,10},{10,8},{9,1... | collective-permute-start | bytes 7077896 | tf_op jit(solution)/shard_map/ppermute | solution.py:85
  98.8 22.5 %collective-permute-start.3 = (bf16[512,768]{1,0:T(8,128)(2,1)}, bf16[512,768]{1,0:T(8,128)(2,1)}, u32[]{:S(2)}, u32[]{:S(2)}) collective-permute-start(bf16[512,768]{1,0:T(8,128)(2,1)} %add_convert_fusion.1), channel_id=1, source_target_pairs={{0,1},{1,0},{2,3},{3,2},{4,5},{5,4},{6,7},{7,6},{8,9},{9,8},{10,11... | collective-permute-start | bytes 2359304 | tf_op jit(solution)/shard_map/ppermute | solution.py:85
  102.9 17.6 %collective-permute-start.4 = (f32[2,768]{1,0:T(2,128)S(1)}, f32[2,768]{1,0:T(2,128)S(1)}, u32[]{:S(2)}, u32[]{:S(2)}) collective-permute-start(f32[2,768]{1,0:T(2,128)S(1)} %add.160), channel_id=1, source_target_pairs={{0,1},{1,0},{2,3},{3,2},{4,5},{5,4},{6,7},{7,6},{8,9},{9,8},{10,11... | collective-permute-start | bytes 18440 | tf_op jit(solution)/shard_map/ppermute | solution.py:85
  128.4 20.7 %collective-permute-start.10 = (bf16[512,768]{1,0:T(8,128)(2,1)}, bf16[512,768]{1,0:T(8,128)(2,1)S(1)}, u32[]{:S(2)}, u32[]{:S(2)}) collective-permute-start(bf16[512,768]{1,0:T(8,128)(2,1)} %get-tuple-element.24.refs_0_), channel_id=1, source_target_pairs={{0,1},{1,0},{2,3},{3,2},{4,5},{5,4},{6,7},{7,6},{8,9},{9,8},{10,11... | collective-permute-start | bytes 2359304 | tf_op jit(solution)/shard_map/ppermute | solution.py:85
  135.3 13.9 %copy-start.9 = (bf16[1,16,48,1536]{3,2,0,1:T(8,128)(2,1)}, bf16[1,16,48,1536]{3,2,0,1:T(8,128)(2,1)S(1)}, u32[]{:S(2)}) copy-start(bf16[1,16,48,1536]{3,2,0,1:T(8,128)(2,1)S(1)} %get-tuple-element.45) | copy-start | bytes 7077892
  155.1 5.3 %collective-permute-start.11 = (f32[6,512]{1,0:T(8,128)S(1)}, f32[6,512]{1,0:T(8,128)S(1)}, u32[]{:S(2)}, u32[]{:S(2)}) collective-permute-start(f32[6,512]{1,0:T(8,128)S(1)} %stack.63), channel_id=1, source_target_pairs={{0,1},{1,0},{2,3},{3,2},{4,5},{5,4},{6,7},{7,6},{8,9},{9,8},{10,11... | collective-permute-start | bytes 36872 | tf_op jit(solution)/shard_map/ppermute | solution.py:85
  156.6 10.9 %collective-permute-start.16 = (bf16[512,768]{1,0:T(8,128)(2,1)}, bf16[512,768]{1,0:T(8,128)(2,1)}, u32[]{:S(2)}, u32[]{:S(2)}) collective-permute-start(bf16[512,768]{1,0:T(8,128)(2,1)} %get-tuple-element.24.refs_0_), channel_id=1, source_target_pairs={{0,2},{2,0},{1,3},{3,1},{4,6},{6,4},{5,7},{7,5},{8,10},{10,8},{9,1... | collective-permute-start | bytes 2359304 | tf_op jit(solution)/shard_map/ppermute | solution.py:85
  156.6 10.9 %collective-permute-start.17 = (bf16[512,768]{1,0:T(8,128)(2,1)}, bf16[512,768]{1,0:T(8,128)(2,1)}, u32[]{:S(2)}, u32[]{:S(2)}) collective-permute-start(bf16[512,768]{1,0:T(8,128)(2,1)} %copy-done.28), channel_id=1, source_target_pairs={{0,2},{2,0},{1,3},{3,1},{4,6},{6,4},{5,7},{7,5},{8,10},{10,8},{9,1... | collective-permute-start | bytes 2359304 | tf_op jit(solution)/shard_map/ppermute | solution.py:85
  167.5 2.4 collective-permute-start.18
  175.8 64.2 %all-to-all-start.2 = ((bf16[16,2,48,768]{3,2,1,0:T(8,128)(2,1)}), bf16[16,2,48,768]{3,2,1,0:T(8,128)(2,1)}, u32[]{:S(2)}, u32[]{:S(2)}) async-start(bf16[16,2,48,768]{3,2,1,0:T(8,128)(2,1)} %shard_map.122), calls=%async_computation.2 | async-start | bytes 4718592 | tf_op jit(solution)/shard_map/all_to_all | solution.py:144
  183.9 21.3 %collective-permute-start.12 = (bf16[512,768]{1,0:T(8,128)(2,1)S(1)}, bf16[512,768]{1,0:T(8,128)(2,1)}, u32[]{:S(2)}, u32[]{:S(2)}) collective-permute-start(bf16[512,768]{1,0:T(8,128)(2,1)S(1)} %convolution_convert_fusion), channel_id=1, source_target_pairs={{0,1},{1,0},{2,3},{3,2},{4,5},{5,4},{6,7},{7,6},{8,9},{9,8},{10,11... | collective-permute-start | bytes 2359304 | tf_op jit(solution)/shard_map/ppermute | solution.py:85
  214.5 20.5 %collective-permute-start.13 = (bf16[512,768]{1,0:T(8,128)(2,1)}, bf16[512,768]{1,0:T(8,128)(2,1)}, u32[]{:S(2)}, u32[]{:S(2)}) collective-permute-start(bf16[512,768]{1,0:T(8,128)(2,1)} %get-tuple-element.27.refs_0_), channel_id=1, source_target_pairs={{0,1},{1,0},{2,3},{3,2},{4,5},{5,4},{6,7},{7,6},{8,9},{9,8},{10,11... | collective-permute-start | bytes 2359304 | tf_op jit(solution)/shard_map/ppermute | solution.py:85
  215.9 19.1 %collective-permute-start.15 = (bf16[512,768]{1,0:T(8,128)(2,1)S(1)}, bf16[512,768]{1,0:T(8,128)(2,1)S(1)}, u32[]{:S(2)}, u32[]{:S(2)}) collective-permute-start(bf16[512,768]{1,0:T(8,128)(2,1)S(1)} %get-tuple-element.21), channel_id=1, source_target_pairs={{0,2},{2,0},{1,3},{3,1},{4,6},{6,4},{5,7},{7,5},{8,10},{10,8},{9,1... | collective-permute-start | bytes 2359304 | tf_op jit(solution)/shard_map/ppermute | solution.py:85
  215.9 20.0 %collective-permute-start.14 = (bf16[512,768]{1,0:T(8,128)(2,1)}, bf16[512,768]{1,0:T(8,128)(2,1)}, u32[]{:S(2)}, u32[]{:S(2)}) collective-permute-start(bf16[512,768]{1,0:T(8,128)(2,1)} %get-tuple-element.27.refs_0_), channel_id=1, source_target_pairs={{0,2},{2,0},{1,3},{3,1},{4,6},{6,4},{5,7},{7,5},{8,10},{10,8},{9,1... | collective-permute-start | bytes 2359304 | tf_op jit(solution)/shard_map/ppermute | solution.py:85
  235.0 18.0 %collective-permute-start.19 = (bf16[512,768]{1,0:T(8,128)(2,1)}, bf16[512,768]{1,0:T(8,128)(2,1)}, u32[]{:S(2)}, u32[]{:S(2)}) collective-permute-start(bf16[512,768]{1,0:T(8,128)(2,1)} %collective-permute-done.13.refs_0_), channel_id=1, source_target_pairs={{0,2},{2,0},{1,3},{3,1},{4,6},{6,4},{5,7},{7,5},{8,10},{10,8},{9,1... | collective-permute-start | bytes 2359304 | tf_op jit(solution)/shard_map/ppermute | solution.py:85
  240.0 26.8 %all-to-all-start.3 = ((bf16[16,1,48,768]{3,2,1,0:T(8,128)(2,1)}), bf16[16,1,48,768]{3,2,1,0:T(8,128)(2,1)S(1)}, u32[]{:S(2)}, u32[]{:S(2)}) async-start(bf16[16,1,48,768]{3,2,1,0:T(8,128)(2,1)} %shard_map.121), calls=%async_computation.3 | async-start | bytes 2359296 | tf_op jit(solution)/shard_map/all_to_all | solution.py:144
  257.1 16.5 %copy-start.29 = (bf16[512,768]{1,0:T(8,128)(2,1)S(1)}, bf16[512,768]{1,0:T(8,128)(2,1)}, u32[]{:S(2)}) copy-start(bf16[512,768]{1,0:T(8,128)(2,1)} %get-tuple-element.27.refs_0_) | copy-start | bytes 2359300
  259.2 14.3 %copy-start.10 = (f32[1,48,768]{2,1,0:T(8,128)}, f32[1,48,768]{2,1,0:T(8,128)S(1)}, u32[]{:S(2)}) copy-start(f32[1,48,768]{2,1,0:T(8,128)S(1)} %get-tuple-element.57) | copy-start | bytes 442372
  266.8 22.6 %all-to-all-start.4 = ((bf16[16,1,48,768]{3,2,1,0:T(8,128)(2,1)}), bf16[16,1,48,768]{3,2,1,0:T(8,128)(2,1)}, u32[]{:S(2)}, u32[]{:S(2)}) async-start(bf16[16,1,48,768]{3,2,1,0:T(8,128)(2,1)} %shard_map.123), calls=%async_computation.4 | async-start | bytes 2359296 | tf_op jit(solution)/shard_map/all_to_all | solution.py:144
  271.2 7.2 %collective-permute-start.24 = (f32[24,768]{1,0:T(8,128)S(1)}, f32[24,768]{1,0:T(8,128)S(1)}, u32[]{:S(2)}, u32[]{:S(2)}) collective-permute-start(f32[24,768]{1,0:T(8,128)S(1)} %get-tuple-element.64), channel_id=1, source_target_pairs={{0,64},{64,0},{1,65},{65,1},{2,66},{66,2},{3,67},{67,3},{4,68},{68... | collective-permute-start | bytes 221192 | tf_op jit(solution)/shard_map/ppermute | solution.py:85
  272.1 6.3 %collective-permute-start.25 = (f32[24,768]{1,0:T(8,128)S(1)}, f32[24,768]{1,0:T(8,128)S(1)}, u32[]{:S(2)}, u32[]{:S(2)}) collective-permute-start(f32[24,768]{1,0:T(8,128)S(1)} %get-tuple-element.63), channel_id=1, source_target_pairs={{0,66},{2,64},{64,2},{66,0},{1,67},{3,65},{65,3},{67,1},{4,70},{6,... | collective-permute-start | bytes 221192 | tf_op jit(solution)/shard_map/ppermute | solution.py:158
  272.1 6.3 %collective-permute-start.26 = (f32[24,768]{1,0:T(8,128)S(1)}, f32[24,768]{1,0:T(8,128)S(1)}, u32[]{:S(2)}, u32[]{:S(2)}) collective-permute-start(f32[24,768]{1,0:T(8,128)S(1)} %select_bitcast_fusion), channel_id=1, source_target_pairs={{0,2},{2,0},{1,3},{3,1},{4,6},{6,4},{5,7},{7,5},{8,10},{10,8},{9,1... | collective-permute-start | bytes 221192 | tf_op jit(solution)/shard_map/ppermute | solution.py:85
  278.3 13.5 %copy-start.12 = (bf16[24,1536]{1,0:T(8,128)(2,1)S(1)}, bf16[24,1536]{1,0:T(8,128)(2,1)}, u32[]{:S(2)}) copy-start(bf16[24,1536]{1,0:T(8,128)(2,1)} %param.11) | copy-start | bytes 221188
  278.3 13.5 %copy-start.21 = (f32[24]{0:T(128)S(1)}, f32[24]{0:T(128)}, u32[]{:S(2)}) copy-start(f32[24]{0:T(128)} %copy-done.20) | copy-start | bytes 292
  278.3 17.2 %copy-start.1 = (bf16[512,1536]{1,0:T(8,128)(2,1)S(1)}, bf16[512,1536]{1,0:T(8,128)(2,1)}, u32[]{:S(2)}) copy-start(bf16[512,1536]{1,0:T(8,128)(2,1)} %param.7) | copy-start | bytes 4718596
  278.3 17.2 %copy-start.5 = (bf16[512,1536]{1,0:T(8,128)(2,1)S(1)}, bf16[512,1536]{1,0:T(8,128)(2,1)}, u32[]{:S(2)}) copy-start(bf16[512,1536]{1,0:T(8,128)(2,1)} %param.13) | copy-start | bytes 4718596
  278.3 17.2 %copy-start.19 = (f32[1,512]{1,0:T(1,128)S(1)}, f32[1,512]{1,0:T(1,128)}, u32[]{:S(2)}) copy-start(f32[1,512]{1,0:T(1,128)} %copy-done.18) | copy-start | bytes 6148
  278.3 17.2 %copy-start.23 = (f32[512]{0:T(512)S(1)}, f32[512]{0:T(512)}, u32[]{:S(2)}) copy-start(f32[512]{0:T(512)} %copy-done.22) | copy-start | bytes 6148
  278.3 17.2 %copy-start.25 = (f32[512]{0:T(512)S(1)}, f32[512]{0:T(512)}, u32[]{:S(2)}) copy-start(f32[512]{0:T(512)} %copy-done.24) | copy-start | bytes 6148
  290.9 4.4 %collective-permute-start.20 = (f32[24,768]{1,0:T(8,128)S(1)}, f32[24,768]{1,0:T(8,128)S(1)}, u32[]{:S(2)}, u32[]{:S(2)}) collective-permute-start(f32[24,768]{1,0:T(8,128)S(1)} %get-tuple-element.68), channel_id=1, source_target_pairs={{0,64},{64,0},{1,65},{65,1},{2,66},{66,2},{3,67},{67,3},{4,68},{68... | collective-permute-start | bytes 221192 | tf_op jit(solution)/shard_map/ppermute | solution.py:85
  292.0 10.6 %collective-permute-start.27 = (f32[24]{0:T(128)S(1)}, f32[24]{0:T(128)S(1)}, u32[]{:S(2)}, u32[]{:S(2)}) collective-permute-start(f32[24]{0:T(128)S(1)} %multiply_reduce_fusion.3), channel_id=1, source_target_pairs={{0,1},{1,0},{2,3},{3,2},{4,5},{5,4},{6,7},{7,6},{8,9},{9,8},{10,11... | collective-permute-start | bytes 296 | tf_op jit(solution)/shard_map/ppermute | solution.py:85
  293.2 9.4 %collective-permute-start.21 = (f32[24,768]{1,0:T(8,128)S(1)}, f32[24,768]{1,0:T(8,128)S(1)}, u32[]{:S(2)}, u32[]{:S(2)}) collective-permute-start(f32[24,768]{1,0:T(8,128)S(1)} %get-tuple-element.67), channel_id=1, source_target_pairs={{0,66},{2,64},{64,2},{66,0},{1,67},{3,65},{65,3},{67,1},{4,70},{6,... | collective-permute-start | bytes 221192 | tf_op jit(solution)/shard_map/ppermute | solution.py:158
  295.4 7.3 %copy-start.14 = (bf16[24,1536]{1,0:T(8,128)(2,1)S(1)}, bf16[24,1536]{1,0:T(8,128)(2,1)}, u32[]{:S(2)}) copy-start(bf16[24,1536]{1,0:T(8,128)(2,1)} %param.10) | copy-start | bytes 221188
  295.4 7.3 %copy-start.26 = (f32[24]{0:T(128)S(1)}, f32[24]{0:T(128)}, u32[]{:S(2)}) copy-start(f32[24]{0:T(128)} %get-tuple-element.88) | copy-start | bytes 292
  295.4 7.2 %collective-permute-start.22 = (f32[24,768]{1,0:T(8,128)S(1)}, f32[24,768]{1,0:T(8,128)S(1)}, u32[]{:S(2)}, u32[]{:S(2)}) collective-permute-start(f32[24,768]{1,0:T(8,128)S(1)} %get-tuple-element.65), channel_id=1, source_target_pairs={{0,2},{2,0},{1,3},{3,1},{4,6},{6,4},{5,7},{7,5},{8,10},{10,8},{9,1... | collective-permute-start | bytes 221192 | tf_op jit(solution)/shard_map/ppermute | solution.py:85
  302.9 5.1 %collective-permute-start.23 = (f32[24]{0:T(128)S(1)}, f32[24]{0:T(128)S(1)}, u32[]{:S(2)}, u32[]{:S(2)}) collective-permute-start(f32[24]{0:T(128)S(1)} %multiply_reduce_fusion.4), channel_id=1, source_target_pairs={{0,1},{1,0},{2,3},{3,2},{4,5},{5,4},{6,7},{7,6},{8,9},{9,8},{10,11... | collective-permute-start | bytes 296 | tf_op jit(solution)/shard_map/ppermute | solution.py:85
  (16 other events, 48.0 us)
where the time goes:
time: 311 us; the launch traced here: 309 us
  waiting for transfers between devices  142 us (46%)
  starting transfers between devices  51.4 us (17%)
  other arithmetic  36.7 us (12%)
  Pallas kernels  36.6 us (12%)
  matrix products  27.8 us (9%)
  local copies, waits for them, and re-layouts  13.3 us (4%)
    ppermute x24, waiting for transfers between devices, exchanged(): return lax.ppermute(value, axis, SWAP)  77.5 us
    all_to_all x2, waiting for transfers between devices, over_planes(): lax.all_to_all(jnp.broadcast_to(rows[None], (planes, *rows.shape)), YZ, 0...  46.9 us
    pallas_call x3, Pallas kernels, heads_call(): pl.pallas_call(kernel, grid=(heads,), in_specs=[spec(o.shape, first) for...  22.6 us
    ppermute x24, starting transfers between devices, exchanged(): return lax.ppermute(value, axis, SWAP)  18.3 us
    all_to_all x3, waiting for transfers between devices, arriving(): return lax.all_to_all(tiles, YZ, 0, 0, tiled=True)  16.1 us
    all_to_all x3, starting transfers between devices, arriving(): return lax.all_to_all(tiles, YZ, 0, 0, tiled=True)  15.6 us
    dot_general x4, matrix products, matmul(): return jnp.dot(left, right, preferred_element_type=F32)  14.6 us
    pallas_call x3, Pallas kernels, products(): pl.pallas_call(product_kernel, grid=(steps,), in_specs=[pl.BlockSpec((tok...  14 us
  transfers between devices with their start and end apart: 33, of which 18 were waited for; matrix products, arithmetic and copies ran while one was open for 20% of the time, Pallas kernels for 10%

commit v1 on v0

--- a/solution.py
+++ b/solution.py
@@ -1,3 +1,5 @@
+import functools
+
 import jax
 import jax.numpy as jnp
 from jax import lax
@@ -106,6 +108,67 @@
     planes = lax.axis_size(Y) * lax.axis_size(Z)
     got = lax.all_to_all(jnp.broadcast_to(rows[None], (planes, *rows.shape)), YZ, 0, 0, tiled=True)
     return got.swapaxes(0, 1) if rows.ndim == 3 else got.reshape(-1, rows.shape[-1])
+
+
+def shifted(value, axis, step):
+    count = lax.axis_size(axis)
+    return lax.ppermute(value, axis, [(i, (i + step) % count) for i in range(count)])
+
+
+def spread(rows):
+    ny, nz = lax.axis_size(Y), lax.axis_size(Z)
+    half = rows.shape[-1] // 2
+    left, right = rows[..., :half], rows[..., half:]
+    left = jnp.stack([left] + [shifted(left, Y, k) for k in range(1, ny)])
+    right = jnp.stack([right] + [shifted(right, Z, k) for k in range(1, nz)])
+    lefts = [left] + [shifted(left, Z, k) for k in range(1, nz)]
+    rights = [right] + [shifted(right, Y, k) for k in range(1, ny)]
+    return lefts, rights
+
+
+def placed_kernel(place_ref, *refs, ny, nz):
+    *pieces, near_ref, far_ref, near_rows, far_rows, part_ref = refs
+    each, half = pieces[0].shape[2:]
+    y, z = place_ref[0], place_ref[1]
+
+    def run(plane_y, plane_z):
+        return pl.ds(pl.multiple_of((plane_y * nz + plane_z) * each, each), each)
+
+    for group, rows_ref in ((0, near_rows), (ny + nz, far_rows)):
+        for ky in range(ny):
+            for kz in range(nz):
+                at = run(lax.rem(y + ny - ky, ny), lax.rem(z + nz - kz, nz))
+                for block in range(2):
+                    rows_ref[block, at, :half] = pieces[group + kz][ky, block]
+                    rows_ref[block, at, half:] = pieces[group + nz + ky][kz, block]
+    step = near_ref.shape[0] // 2
+
+    @pl.loop(0, 2)
+    def _(i):
+        at = pl.ds(pl.multiple_of(i * step, step), step)
+        part = contract_last(near_ref[at, :], near_rows[0])
+        part = part + contract_last(far_ref[at, :], far_rows[0])
+        part_ref[at, :] = part.astype(BF16)
+
+
+def placed(near, far, hidden_near, hidden_far):
+    nz, ny = len(near[0]), len(near[1])
+    pieces = (*near[0], *near[1], *far[0], *far[1])
+    each, half = pieces[0].shape[2:]
+    count = ny * nz * each
+    tokens = hidden_near.shape[0]
+    place = jnp.stack((lax.axis_index(Y), lax.axis_index(Z))).astype(jnp.int32)
+    vmem = pl.BlockSpec(memory_space=pltpu.VMEM)
+    rows = jax.ShapeDtypeStruct((2, count, 2 * half), BF16)
+    return pl.pallas_call(
+        functools.partial(placed_kernel, ny=ny, nz=nz),
+        in_specs=[pl.BlockSpec(memory_space=pltpu.SMEM)] + [vmem] * (len(pieces) + 2),
+        out_specs=[vmem] * 3,
+        out_shape=[rows, rows, jax.ShapeDtypeStruct((tokens, count), BF16)],
+        cost_estimate=pl.CostEstimate(
+            flops=8 * tokens * count * half, bytes_accessed=16 * count * half, transcendentals=0
+        ),
+    )(place, *pieces, hidden_near, hidden_far)
 
 
 def product_kernel(*refs):
@@ -174,9 +237,13 @@
     pair_v = jnp.stack((chosen(at_own, next_v, w_value), chosen(at_own, w_value, next_v)))
     other_v = exchanged(columns(pair_v, 1 - core), C)
     pair_v = in_order(core, columns(pair_v, core), other_v, 1)
-    raw_near = over_planes(pair_v)
-    raw_far = exchanged(raw_near, C)
-    raw_near, raw_far = (w.reshape(2, width, -1) for w in (raw_near, raw_far))
+    pieces = spread(pair_v)
+    pieces_far = tuple([exchanged(p, C) for p in group] for group in pieces)
+
+    hidden_near, hidden_far = lax.optimization_barrier(
+        (columns(hidden, core), columns(hidden, 1 - core))
+    )
+    raw_near, raw_far, part = placed(pieces, pieces_far, hidden_near, hidden_far)
 
     next_o = exchanged(w_out, X)
     own_vf, own_of = w_value.astype(F32), w_out.astype(F32)
@@ -193,7 +260,6 @@
     send_o = columns(pair_o, 1 - core)
     other_o = exchanged(send_o, C)
     pair_o = in_order(core, columns(pair_o, core), other_o, 1)
-    pair_o, _ = lax.optimization_barrier((pair_o, raw_near))
     both_o = over_planes(pair_o)
     both_o_far = exchanged(both_o, C)
     weight_o = in_order(core, both_o, both_o_far, 3)
@@ -203,13 +269,8 @@
     (probs,) = heads_call(
         probs_kernel, heads, ((queries, 0), (attn_keys, 0)), (((heads, tokens, tokens), F32, 0),), 1
     )
-    hidden_near, hidden_far = lax.optimization_barrier(
-        (columns(hidden, core), columns(hidden, 1 - core))
-    )
     hidden_other = exchanged(hidden_far, C)
     full = (tokens, width)
-    part = contract_last(hidden_near, raw_near[0]) + contract_last(hidden_far, raw_far[0])
-    part = part.astype(BF16)
     value_peer = exchanged(part)
     value_own = contract_last(hidden_near, raw_near[1]) + contract_last(hidden_far, raw_far[1])
     near, far, _ = lax.optimization_barrier((raw_near, raw_far, part))
@@ -291,7 +352,7 @@
     tiles = products((gv_peer, gv_peer_other), hidden_near, hidden_other, 2 * rows)
     gw_v_peer = summed(arriving(tiles, at_own_v))[0]
     from_own = lax.optimization_barrier(matmul(gv_own, weight_v_own))
-    from_peer = matmul(gv_peer, weight_v_peer)
+    from_peer = lax.optimization_barrier(matmul(gv_peer, weight_v_peer))
     grad_hidden = (grad_res + from_own + from_peer).astype(BF16)
     gw_o_mine, dot_o = owned(gw_o[0], gw_o[1], at_own, core, unit_o)
     gw_v_mine, dot_v = owned(gw_v_own, gw_v_peer, at_own, core, unit_v)

time: 311 us -> 315 us (1.013)
  starting transfers between devices: 51.4 us -> 79.2 us
  waiting for transfers between devices: 142 us -> 118 us
  matrix products: 27.8 us -> 19.9 us
  Pallas kernels: 36.6 us -> 43.1 us
  local copies, waits for them, and re-layouts: 13.3 us -> 7.37 us
  other arithmetic: 36.7 us -> 42.4 us
    all_to_all x2 -> x1, waiting for transfers between devices: 46.9 us -> 0.01 us  [over_planes(): lax.all_to_all(jnp.broadcast_to(rows[None], (planes, *rows.shape)), YZ, 0...]
    ppermute x0 -> x12, waiting for transfers between devices: none -> 32.4 us  [shifted(): lax.ppermute(value, axis, [(i, (i + step) % count) for i in range(count)])]
    ppermute x0 -> x12, starting transfers between devices: none -> 25.5 us  [shifted(): lax.ppermute(value, axis, [(i, (i + step) % count) for i in range(count)])]
    ppermute x24 -> x31, starting transfers between devices: 18.3 us -> 25.5 us  [exchanged(): return lax.ppermute(value, axis, SWAP)]
    ppermute x24 -> x31, waiting for transfers between devices: 77.5 us -> 70.5 us  [exchanged(): return lax.ppermute(value, axis, SWAP)]
    pallas_call x0 -> x1, Pallas kernels: none -> 6.5 us  [placed(): pl.pallas_call(functools.partial(placed_kernel, ny=ny, nz=nz), in_specs=[...]
    convert_element_type x0 -> x1, other arithmetic: none -> 5.32 us  [shards(): grad_hidden = (grad_res + from_own + from_peer).astype(BF16)]
    all_to_all x2 -> x1, starting transfers between devices: 13.3 us -> 8.22 us  [over_planes(): lax.all_to_all(jnp.broadcast_to(rows[None], (planes, *rows.shape)), YZ, 0...]
  transfers between devices with their start and end apart: 33 -> 51, of which waited for: 18 -> 20; matrix products, arithmetic and copies ran while one was open for 20% -> 18% of each run, Pallas kernels for 10% -> 12%
where the time goes in v1:
time: 315 us; the launch traced here: 311 us
  waiting for transfers between devices  118 us (37%)
  starting transfers between devices  79.2 us (25%)
  Pallas kernels  43.1 us (14%)
  other arithmetic  42.4 us (13%)
  matrix products  19.9 us (6%)
  local copies, waits for them, and re-layouts  7.37 us (2%)
    ppermute x31, waiting for transfers between devices, exchanged(): return lax.ppermute(value, axis, SWAP)  70.5 us
    ppermute x12, waiting for transfers between devices, shifted(): lax.ppermute(value, axis, [(i, (i + step) % count) for i in range(count)])  32.4 us
    ppermute x12, starting transfers between devices, shifted(): lax.ppermute(value, axis, [(i, (i + step) % count) for i in range(count)])  25.5 us
    ppermute x31, starting transfers between devices, exchanged(): return lax.ppermute(value, axis, SWAP)  25.5 us
    pallas_call x3, Pallas kernels, heads_call(): pl.pallas_call(kernel, grid=(heads,), in_specs=[spec(o.shape, first) for...  22.6 us
    all_to_all x3, starting transfers between devices, arriving(): return lax.all_to_all(tiles, YZ, 0, 0, tiled=True)  16.6 us
    pallas_call x3, Pallas kernels, products(): pl.pallas_call(product_kernel, grid=(steps,), in_specs=[pl.BlockSpec((tok...  14.1 us
    all_to_all x3, waiting for transfers between devices, arriving(): return lax.all_to_all(tiles, YZ, 0, 0, tiled=True)  12.2 us
  transfers between devices with their start and end apart: 51, of which 20 were waited for; matrix products, arithmetic and copies ran while one was open for 18% of the time, Pallas kernels for 12%

profile of v1, /device:TPU:6, one launch (start us, length us, event | category | flops | bytes accessed | tf_op | source)
XLA Modules:
  0.0 311.4 jit_solution(16907040382437956617)
XLA Ops:
  4.8 2.2 collective-permute-start.24
  7.0 3.0 collective-permute-done.24
  14.2 8.2 %all-to-all-start = ((bf16[16,2,48,768]{3,2,1,0:T(8,128)(2,1)}), bf16[16,2,48,768]{3,2,1,0:T(8,128)(2,1)}, u32[]{:S(2)}, u32[]{:S(2)}) async-start(bf16[16,2,48,768]{3,2,1,0:T(8,128)(2,1)} %broadcast_in_dim.8), calls=%async_computation | async-start | bytes 4718592 | tf_op jit(solution)/shard_map/all_to_all | solution.py:109
  22.6 4.3 %collective-permute-done = bf16[24,1536]{1,0:T(8,128)(2,1)S(1)} collective-permute-done((bf16[24,1536]{1,0:T(8,128)(2,1)S(1)}, bf16[24,1536]{1,0:T(8,128)(2,1)S(1)}, u32[]{:S(2)}, u32[]{:S(2)}) %collective-permute-start) | collective-permute-done | bytes 73760 | tf_op jit(solution)/shard_map/ppermute | solution.py:87
  28.4 3.2 %collective-permute-start.4 = (bf16[2,48,384]{2,1,0:T(8,128)(2,1)S(1)}, bf16[2,48,384]{2,1,0:T(8,128)(2,1)S(1)}, u32[]{:S(2)}, u32[]{:S(2)}) collective-permute-start(bf16[2,48,384]{2,1,0:T(8,128)(2,1)S(1)} %get-tuple-element.74), channel_id=1, source_target_pairs={{0,48},{16,0},{32,16},{48,32},{1,49},{17,1},{33,17},{49,33},{2,50}... | collective-permute-start | bytes 221192 | tf_op jit(solution)/shard_map/ppermute | solution.py:115
  33.2 20.0 %collective-permute-done.4 = bf16[2,48,384]{2,1,0:T(8,128)(2,1)S(1)} collective-permute-done((bf16[2,48,384]{2,1,0:T(8,128)(2,1)S(1)}, bf16[2,48,384]{2,1,0:T(8,128)(2,1)S(1)}, u32[]{:S(2)}, u32[]{:S(2)}) %collective-permute-start.4) | collective-permute-done | bytes 73760 | tf_op jit(solution)/shard_map/ppermute | solution.py:115
  53.2 2.9 collective-permute-done.3
  61.1 2.8 collective-permute-start.6
  65.7 3.5 %collective-permute-done.9 = bf16[2,48,384]{2,1,0:T(8,128)(2,1)S(1)} collective-permute-done((bf16[2,48,384]{2,1,0:T(8,128)(2,1)S(1)}, bf16[2,48,384]{2,1,0:T(8,128)(2,1)S(1)}, u32[]{:S(2)}, u32[]{:S(2)}) %collective-permute-start.9) | collective-permute-done | bytes 73760 | tf_op jit(solution)/shard_map/ppermute | solution.py:115
  70.3 8.4 %collective-permute-start.11 = (bf16[4,2,48,384]{3,2,1,0:T(8,128)(2,1)S(1)}, bf16[4,2,48,384]{3,2,1,0:T(8,128)(2,1)S(1)}, u32[]{:S(2)}, u32[]{:S(2)}) collective-permute-start(bf16[4,2,48,384]{3,2,1,0:T(8,128)(2,1)S(1)} %pad_maximum_fusion.1.refs_4_), channel_id=1, source_target_pairs={{0,16},{16,32},{32,48},{48,0},{1,17},{17,33},{33,49},{49,1},{2,18}... | collective-permute-start | bytes 884744 | tf_op jit(solution)/shard_map/ppermute | solution.py:115
  78.7 2.8 collective-permute-start.13
  82.9 4.1 %collective-permute-done.12.refs_6_ = bf16[4,2,48,384]{3,2,1,0:T(8,128)(2,1)} collective-permute-done((bf16[4,2,48,384]{3,2,1,0:T(8,128)(2,1)S(1)}, bf16[4,2,48,384]{3,2,1,0:T(8,128)(2,1)}, u32[]{:S(2)}, u32[]{:S(2)}) %collective-permute-start.12) | collective-permute-done | bytes 294944 | tf_op jit(solution)/shard_map/ppermute | solution.py:115
  90.5 6.9 %shard_map.118.p_ref = f32[6,512,512]{2,1,0:T(8,128)} custom-call(bf16[512,768]{1,0:T(8,128)(2,1)} %q_ref.3, bf16[512,768]{1,0:T(8,128)(2,1)} %k_ref.3), custom_call_target="tpu_custom_call" | custom-call | flops 805306368 | bytes 10223616 | tf_op jit(solution)/shard_map/pallas_call | solution.py:71
  99.0 6.5 %shard_map.119 = (bf16[2,768,768]{2,1,0:T(8,128)(2,1)}, bf16[2,768,768]{2,1,0:T(8,128)(2,1)}, bf16[512,768]{1,0:T(8,128)(2,1)}) custom-call(s32[2]{0:T(128)} %pad_add_fusion.place_ref, bf16[4,2,48,384]{3,2,1,0:T(8,128)(2,1)} %copy-done.14, bf16[4,2,48,384]{3,2,1,0:T(8,128)(2,1)} %copy-done.20, bf16[4,2,48,384]{3,2,1,0:T(8,128)(2,1)} %copy-done.21, ...), custom_call_target="tpu_custom_call" | custom-call | flops 1207959552 | bytes 4718592 | tf_op jit(solution)/shard_map/pallas_call | solution.py:163
  105.5 2.4 collective-permute-start.22
  107.9 3.5 %multiply_reduce_fusion = (f32[2,768]{1,0:T(2,128)S(1)}, f32[2,768]{1,0:T(2,128)S(1)}) fusion(bf16[2,768,768]{2,1,0:T(8,128)(2,1)} %get-tuple-element.30, bf16[2,768,768]{2,1,0:T(8,128)(2,1)} %get-tuple-element.29), kind=kLoop, calls=%fused_computation.14 | loop fusion | flops 7074816 | bytes 4730880 | tf_op jit(solution)/shard_map/reduce_sum | solution.py:278
  115.8 11.4 %collective-permute-done.23 = f32[2,768]{1,0:T(2,128)S(1)} collective-permute-done((f32[2,768]{1,0:T(2,128)S(1)}, f32[2,768]{1,0:T(2,128)S(1)}, u32[]{:S(2)}, u32[]{:S(2)}) %collective-permute-start.23) | collective-permute-done | bytes 6176 | tf_op jit(solution)/shard_map/ppermute | solution.py:87
  128.3 6.5 %shard_map.120 = (bf16[512,768]{1,0:T(8,128)(2,1)}, bf16[512,768]{1,0:T(8,128)(2,1)}) custom-call(f32[6,512,512]{2,1,0:T(8,128)} %shard_map.118.p_ref, f32[512,768]{1,0:T(8,128)} %convolution_add_fusion.own_ref, bf16[512,768]{1,0:T(8,128)(2,1)} %copy-done.18, f32[8,768]{1,0:T(8,128)} %broadcast_in_dim.7.rate_ref), custom_call_target="tpu_custom_call" | custom-call | flops 805306368 | bytes 10223616 | tf_op jit(solution)/shard_map/pallas_call | solution.py:71
  136.9 4.9 %maximum_select_fusion = bf16[2,16,48,1536]{3,2,0,1:T(8,128)(2,1)S(1)} fusion(bf16[2,16,48,768]{3,2,0,1:T(8,128)(2,1)} %collective-permute-done.28, bf16[2,16,48,768]{3,2,0,1:T(8,128)(2,1)} %bitcast.19, pred[]{:T(512)S(6)} %eq.6), kind=kLoop, calls=%fused_computation.11 | loop fusion | flops 21233664 | bytes 9437185 | tf_op jit(solution)/shard_map/jit(_where)/select_n | solution.py:100
  144.3 10.8 %collective-permute-done.29.refs_2_ = bf16[512,768]{1,0:T(8,128)(2,1)S(1)} collective-permute-done((bf16[512,768]{1,0:T(8,128)(2,1)}, bf16[512,768]{1,0:T(8,128)(2,1)S(1)}, u32[]{:S(2)}, u32[]{:S(2)}) %collective-permute-start.29) | collective-permute-done | bytes 786464 | tf_op jit(solution)/shard_map/ppermute | solution.py:87
  157.3 2.8 fusion.2
  160.1 2.2 collective-permute-start.30
  162.8 2.6 collective-permute-done.30
  165.5 3.5 %multiply_convert_fusion = bf16[512,1536]{1,0:T(8,128)(2,1)S(1)} fusion(f32[512,1536]{1,0:T(8,128)S(1)} %get-tuple-element.48, bf16[512,1536]{1,0:T(8,128)(2,1)} %param.13, f32[512]{0:T(512)S(1)} %get-tuple-element.87, f32[512]{0:T(512)S(1)} %get-tuple-element.91, f32[512]{0:T(512)S(1)} %get-tuple-element.88, f32[512]{0:T(512)S(1)} %bitcast.84, ...), kind=kLoop, calls=%fused_computation.27 | loop fusion | flops 13369344 | bytes 7878656 | tf_op jit(solution)/shard_map/convert_element_type | solution.py:326
  171.1 2.4 collective-permute-done.37.refs_5_
  173.5 5.9 %shard_map.123 = bf16[16,2,48,768]{3,2,1,0:T(8,128)(2,1)} custom-call(bf16[512,768]{1,0:T(8,128)(2,1)} %get-tuple-element.31.refs_0_, bf16[512,768]{1,0:T(8,128)(2,1)} %collective-permute-done.35.refs_1_, bf16[512,768]{1,0:T(8,128)(2,1)} %copy-done.30, bf16[512,768]{1,0:T(8,128)(2,1)} %collective-permute-done.36.refs_3_, ...), custom_call_target="tpu_custom_call" | custom-call | flops 2415919104 | bytes 2359296 | tf_op jit(solution)/shard_map/pallas_call | solution.py:188
  179.4 5.6 %all-to-all-start.1 = ((bf16[16,2,48,768]{3,2,1,0:T(8,128)(2,1)}), bf16[16,2,48,768]{3,2,1,0:T(8,128)(2,1)}, u32[]{:S(2)}, u32[]{:S(2)}) async-start(bf16[16,2,48,768]{3,2,1,0:T(8,128)(2,1)} %shard_map.123), calls=%async_computation.1 | async-start | bytes 4718592 | tf_op jit(solution)/shard_map/all_to_all | solution.py:207
  185.0 3.7 %convolution_convert_fusion = bf16[512,768]{1,0:T(8,128)(2,1)S(1)} fusion(bf16[512,1536]{1,0:T(8,128)(2,1)} %copy-done.7, bf16[768,1536]{1,0:T(8,128)(2,1)} %bitcast.76), kind=kOutput, calls=%fused_computation.36 | convolution fusion | flops 1208352768 | bytes 4718592 | tf_op jit(solution)/shard_map/dot_general | solution.py:25
  188.7 2.4 collective-permute-start.31
  191.2 2.6 fusion.39.own_ref
  193.7 16.2 %collective-permute-done.31.peer_ref = bf16[512,768]{1,0:T(8,128)(2,1)} collective-permute-done((bf16[512,768]{1,0:T(8,128)(2,1)S(1)}, bf16[512,768]{1,0:T(8,128)(2,1)}, u32[]{:S(2)}, u32[]{:S(2)}) %collective-permute-start.31) | collective-permute-done | bytes 786464 | tf_op jit(solution)/shard_map/ppermute | solution.py:87
  209.9 9.2 %shard_map.121 = (bf16[512,768]{1,0:T(8,128)(2,1)}, bf16[512,768]{1,0:T(8,128)(2,1)}, bf16[512,768]{1,0:T(8,128)(2,1)}) custom-call(bf16[512,768]{1,0:T(8,128)(2,1)} %q_ref.3, bf16[512,768]{1,0:T(8,128)(2,1)} %k_ref.3, bf16[512,768]{1,0:T(8,128)(2,1)} %get-tuple-element.32.v_ref, f32[6,512,512]{2,1,0:T(8,128)} %shard_map.118.p_ref, ...), custom_call_target="tpu_custom_call" | custom-call | flops 3221225472 | bytes 10223616 | tf_op jit(solution)/shard_map/pallas_call | solution.py:71
  219.2 2.2 collective-permute-start.32
  221.9 17.6 %collective-permute-done.32.refs_0_ = bf16[512,768]{1,0:T(8,128)(2,1)} collective-permute-done((bf16[512,768]{1,0:T(8,128)(2,1)}, bf16[512,768]{1,0:T(8,128)(2,1)}, u32[]{:S(2)}, u32[]{:S(2)}) %collective-permute-start.32) | collective-permute-done | bytes 786464 | tf_op jit(solution)/shard_map/ppermute | solution.py:87
  239.4 4.1 %shard_map.122 = bf16[16,1,48,768]{3,2,1,0:T(8,128)(2,1)} custom-call(bf16[512,768]{1,0:T(8,128)(2,1)} %get-tuple-element.33.refs_0_, bf16[512,768]{1,0:T(8,128)(2,1)} %collective-permute-done.33.refs_1_, bf16[512,768]{1,0:T(8,128)(2,1)} %get-tuple-element.24.refs_16_.refs_2_, bf16[512,768]{1,0:T(8,128)(2,1)} %collective-permute-done.34.refs_3_), custom_call_target="tpu_custom_call" | custom-call | flops 1207959552 | bytes 2359296 | tf_op jit(solution)/shard_map/pallas_call | solution.py:188
  243.5 6.7 %all-to-all-start.2 = ((bf16[16,1,48,768]{3,2,1,0:T(8,128)(2,1)}), bf16[16,1,48,768]{3,2,1,0:T(8,128)(2,1)}, u32[]{:S(2)}, u32[]{:S(2)}) async-start(bf16[16,1,48,768]{3,2,1,0:T(8,128)(2,1)} %shard_map.122), calls=%async_computation.2 | async-start | bytes 2359296 | tf_op jit(solution)/shard_map/all_to_all | solution.py:207
  250.2 5.0 %divide_convert_fusion = bf16[2,768,1536]{2,1,0:T(8,128)(2,1)S(1)} fusion(bf16[2,768,768]{2,1,0:T(8,128)(2,1)} %get-tuple-element.30, bf16[2,768,768]{2,1,0:T(8,128)(2,1)} %get-tuple-element.29, f32[2,768]{1,0:T(2,128)S(1)} %get-tuple-element.46, pred[]{:T(512)S(6)} %eq.6), kind=kLoop, calls=%fused_computation | loop fusion | flops 28311552 | bytes 9443329 | tf_op jit(solution)/shard_map/convert.1
  255.3 3.1 %fusion.11 = f32[512,1536]{1,0:T(8,128)} fusion(bf16[512,768]{1,0:T(8,128)(2,1)S(1)} %copy-done.31, bf16[2,768,1536]{2,1,0:T(8,128)(2,1)S(1)} %divide_convert_fusion), kind=kOutput, calls=%fused_computation.32 | convolution fusion | flops 1207959552 | bytes 6291456 | tf_op jit(solution)/shard_map/dot_general | solution.py:33
  258.4 4.1 %shard_map.124 = bf16[16,1,48,768]{3,2,1,0:T(8,128)(2,1)} custom-call(bf16[512,768]{1,0:T(8,128)(2,1)} %collective-permute-done.32.refs_0_, bf16[512,768]{1,0:T(8,128)(2,1)} %collective-permute-done.38.refs_1_, bf16[512,768]{1,0:T(8,128)(2,1)} %get-tuple-element.24.refs_16_.refs_2_, bf16[512,768]{1,0:T(8,128)(2,1)} %collective-permute-done.34.refs_3_), custom_call_target="tpu_custom_call" | custom-call | flops 1207959552 | bytes 2359296 | tf_op jit(solution)/shard_map/pallas_call | solution.py:188
  265.2 5.1 %all-to-all-done.2 = bf16[16,1,48,768]{3,2,1,0:T(8,128)(2,1)} async-done(((bf16[16,1,48,768]{3,2,1,0:T(8,128)(2,1)}), bf16[16,1,48,768]{3,2,1,0:T(8,128)(2,1)}, u32[]{:S(2)}, u32[]{:S(2)}) %all-to-all-start.2) | async-done | bytes 1179680 | tf_op jit(solution)/shard_map/all_to_all | solution.py:207
  270.3 4.4 %all-to-all-start.3 = ((bf16[16,1,48,768]{3,2,1,0:T(8,128)(2,1)}), bf16[16,1,48,768]{3,2,1,0:T(8,128)(2,1)}, u32[]{:S(2)}, u32[]{:S(2)}) async-start(bf16[16,1,48,768]{3,2,1,0:T(8,128)(2,1)} %shard_map.124), calls=%async_computation.3 | async-start | bytes 2359296 | tf_op jit(solution)/shard_map/all_to_all | solution.py:207
  277.9 5.0 %fusion.10 = f32[512,1536]{1,0:T(8,128)} fusion(bf16[512,768]{1,0:T(8,128)(2,1)} %collective-permute-done.32.refs_0_, bf16[2,768,1536]{2,1,0:T(8,128)(2,1)} %copy-done.9), kind=kOutput, calls=%fused_computation.30 | convolution fusion | flops 1207959552 | bytes 6291456 | tf_op jit(solution)/shard_map/dot_general | solution.py:33
  283.6 2.1 convert_reduce_fusion.2
  285.7 7.1 %all-to-all-done.3 = bf16[16,1,48,768]{3,2,1,0:T(8,128)(2,1)} async-done(((bf16[16,1,48,768]{3,2,1,0:T(8,128)(2,1)}), bf16[16,1,48,768]{3,2,1,0:T(8,128)(2,1)}, u32[]{:S(2)}, u32[]{:S(2)}) %all-to-all-start.3) | async-done | bytes 1179680 | tf_op jit(solution)/shard_map/all_to_all | solution.py:207
  295.8 3.5 %collective-permute-start.46 = (f32[24]{0:T(128)S(1)}, f32[24]{0:T(128)S(1)}, u32[]{:S(2)}, u32[]{:S(2)}) collective-permute-start(f32[24]{0:T(128)S(1)} %multiply_reduce_fusion.3), channel_id=1, source_target_pairs={{0,1},{1,0},{2,3},{3,2},{4,5},{5,4},{6,7},{7,6},{8,9},{9,8},{10,11... | collective-permute-start | bytes 296 | tf_op jit(solution)/shard_map/ppermute | solution.py:87
  300.0 5.3 %add_convert_fusion = (bf16[512,1536]{1,0:T(8,128)(2,1)}, bf16[512,1536]{1,0:T(8,128)(2,1)}) fusion(f32[512,1536]{1,0:T(8,128)} %fusion.10, f32[512,1536]{1,0:T(8,128)} %fusion.11, bf16[512,1536]{1,0:T(8,128)(2,1)} %param.13, f32[512]{0:T(512)S(1)} %get-tuple-element.91, f32[512]{0:T(512)S(1)} %get-tuple-element.88, f32[1536]{0:T(1024)S(1)} %get-tuple-element.89, ...), kind=kLoop, calls=%fused_computation.26 | loop fusion | flops 12582912 | bytes 15747072 | tf_op jit(solution)/shard_map/convert_element_type | solution.py:356
  305.5 2.2 collective-permute-start.42
  308.5 2.1 collective-permute-done.42
  (188 shorter events, 53.2 us)
Async XLA Ops:
  0.6 9.4 %collective-permute-start.25 = (bf16[24,1536]{1,0:T(8,128)(2,1)}, bf16[24,1536]{1,0:T(8,128)(2,1)S(1)}, u32[]{:S(2)}, u32[]{:S(2)}) collective-permute-start(bf16[24,1536]{1,0:T(8,128)(2,1)} %param.11), channel_id=1, source_target_pairs={{0,64},{64,0},{1,65},{65,1},{2,66},{66,2},{3,67},{67,3},{4,68},{68... | collective-permute-start | bytes 221192 | tf_op jit(solution)/shard_map/ppermute | solution.py:87
  2.6 7.6 %collective-permute-start.26 = (f32[24]{0:T(128)S(1)}, f32[24]{0:T(128)S(1)}, u32[]{:S(2)}, u32[]{:S(2)}) collective-permute-start(f32[24]{0:T(128)S(1)} %fusion.17), channel_id=1, source_target_pairs={{0,65},{1,64},{64,1},{65,0},{2,67},{3,66},{66,3},{67,2},{4,69},{5,... | collective-permute-start | bytes 296 | tf_op jit(solution)/shard_map/ppermute | solution.py:254
  4.8 5.2 %collective-permute-start.24 = (f32[2,24]{1,0:T(2,128)S(1)}, f32[2,24]{1,0:T(2,128)S(1)}, u32[]{:S(2)}, u32[]{:S(2)}) collective-permute-start(f32[2,24]{1,0:T(2,128)S(1)} %pad_maximum_fusion.4), channel_id=1, source_target_pairs={{0,1},{1,0},{2,3},{3,2},{4,5},{5,4},{6,7},{7,6},{8,9},{9,8},{10,11... | collective-permute-start | bytes 584 | tf_op jit(solution)/shard_map/ppermute | solution.py:253
  14.2 67.2 %all-to-all-start = ((bf16[16,2,48,768]{3,2,1,0:T(8,128)(2,1)}), bf16[16,2,48,768]{3,2,1,0:T(8,128)(2,1)}, u32[]{:S(2)}, u32[]{:S(2)}) async-start(bf16[16,2,48,768]{3,2,1,0:T(8,128)(2,1)} %broadcast_in_dim.8), calls=%async_computation | async-start | bytes 4718592 | tf_op jit(solution)/shard_map/all_to_all | solution.py:109
  22.4 4.4 %collective-permute-start = (bf16[24,1536]{1,0:T(8,128)(2,1)S(1)}, bf16[24,1536]{1,0:T(8,128)(2,1)S(1)}, u32[]{:S(2)}, u32[]{:S(2)}) collective-permute-start(bf16[24,1536]{1,0:T(8,128)(2,1)S(1)} %copy-done.17), channel_id=1, source_target_pairs={{0,64},{64,0},{1,65},{65,1},{2,66},{66,2},{3,67},{67,3},{4,68},{68... | collective-permute-start | bytes 221192 | tf_op jit(solution)/shard_map/ppermute | solution.py:87
  28.4 24.9 %collective-permute-start.4 = (bf16[2,48,384]{2,1,0:T(8,128)(2,1)S(1)}, bf16[2,48,384]{2,1,0:T(8,128)(2,1)S(1)}, u32[]{:S(2)}, u32[]{:S(2)}) collective-permute-start(bf16[2,48,384]{2,1,0:T(8,128)(2,1)S(1)} %get-tuple-element.74), channel_id=1, source_target_pairs={{0,48},{16,0},{32,16},{48,32},{1,49},{17,1},{33,17},{49,33},{2,50}... | collective-permute-start | bytes 221192 | tf_op jit(solution)/shard_map/ppermute | solution.py:115
  31.5 24.6 %collective-permute-start.3 = (bf16[2,48,384]{2,1,0:T(8,128)(2,1)S(1)}, bf16[2,48,384]{2,1,0:T(8,128)(2,1)S(1)}, u32[]{:S(2)}, u32[]{:S(2)}) collective-permute-start(bf16[2,48,384]{2,1,0:T(8,128)(2,1)S(1)} %get-tuple-element.74), channel_id=1, source_target_pairs={{0,32},{16,48},{32,0},{48,16},{1,33},{17,49},{33,1},{49,17},{2,34}... | collective-permute-start | bytes 221192 | tf_op jit(solution)/shard_map/ppermute | solution.py:115
  32.4 23.8 %collective-permute-start.2 = (bf16[2,48,384]{2,1,0:T(8,128)(2,1)S(1)}, bf16[2,48,384]{2,1,0:T(8,128)(2,1)S(1)}, u32[]{:S(2)}, u32[]{:S(2)}) collective-permute-start(bf16[2,48,384]{2,1,0:T(8,128)(2,1)S(1)} %get-tuple-element.74), channel_id=1, source_target_pairs={{0,16},{16,32},{32,48},{48,0},{1,17},{17,33},{33,49},{49,1},{2,18}... | collective-permute-start | bytes 221192 | tf_op jit(solution)/shard_map/ppermute | solution.py:115
  56.2 22.5 %collective-permute-start.5 = (bf16[4,2,48,384]{3,2,1,0:T(8,128)(2,1)S(1)}, bf16[4,2,48,384]{3,2,1,0:T(8,128)(2,1)S(1)}, u32[]{:S(2)}, u32[]{:S(2)}) collective-permute-start(bf16[4,2,48,384]{3,2,1,0:T(8,128)(2,1)S(1)} %pad_maximum_fusion.refs_0_), channel_id=1, source_target_pairs={{0,4},{4,8},{8,12},{12,0},{1,5},{5,9},{9,13},{13,1},{2,6},{6,10},{... | collective-permute-start | bytes 884744 | tf_op jit(solution)/shard_map/ppermute | solution.py:115
  57.7 6.2 %collective-permute-start.10 = (bf16[2,48,384]{2,1,0:T(8,128)(2,1)S(1)}, bf16[2,48,384]{2,1,0:T(8,128)(2,1)S(1)}, u32[]{:S(2)}, u32[]{:S(2)}) collective-permute-start(bf16[2,48,384]{2,1,0:T(8,128)(2,1)S(1)} %get-tuple-element.73), channel_id=1, source_target_pairs={{0,12},{4,0},{8,4},{12,8},{1,13},{5,1},{9,5},{13,9},{2,14},{6,2},{... | collective-permute-start | bytes 221192 | tf_op jit(solution)/shard_map/ppermute | solution.py:115
  59.5 9.7 %collective-permute-start.9 = (bf16[2,48,384]{2,1,0:T(8,128)(2,1)S(1)}, bf16[2,48,384]{2,1,0:T(8,128)(2,1)S(1)}, u32[]{:S(2)}, u32[]{:S(2)}) collective-permute-start(bf16[2,48,384]{2,1,0:T(8,128)(2,1)S(1)} %get-tuple-element.73), channel_id=1, source_target_pairs={{0,8},{4,12},{8,0},{12,4},{1,9},{5,13},{9,1},{13,5},{2,10},{6,14},... | collective-permute-start | bytes 221192 | tf_op jit(solution)/shard_map/ppermute | solution.py:115
  60.6 9.6 %collective-permute-start.8 = (bf16[2,48,384]{2,1,0:T(8,128)(2,1)S(1)}, bf16[2,48,384]{2,1,0:T(8,128)(2,1)S(1)}, u32[]{:S(2)}, u32[]{:S(2)}) collective-permute-start(bf16[2,48,384]{2,1,0:T(8,128)(2,1)S(1)} %get-tuple-element.73), channel_id=1, source_target_pairs={{0,4},{4,8},{8,12},{12,0},{1,5},{5,9},{9,13},{13,1},{2,6},{6,10},{... | collective-permute-start | bytes 221192 | tf_op jit(solution)/shard_map/ppermute | solution.py:115
  61.1 20.4 %collective-permute-start.6 = (bf16[4,2,48,384]{3,2,1,0:T(8,128)(2,1)S(1)}, bf16[4,2,48,384]{3,2,1,0:T(8,128)(2,1)S(1)}, u32[]{:S(2)}, u32[]{:S(2)}) collective-permute-start(bf16[4,2,48,384]{3,2,1,0:T(8,128)(2,1)S(1)} %pad_maximum_fusion.refs_0_), channel_id=1, source_target_pairs={{0,8},{4,12},{8,0},{12,4},{1,9},{5,13},{9,1},{13,5},{2,10},{6,14},... | collective-permute-start | bytes 884744 | tf_op jit(solution)/shard_map/ppermute | solution.py:115
  63.9 17.6 %collective-permute-start.7 = (bf16[4,2,48,384]{3,2,1,0:T(8,128)(2,1)S(1)}, bf16[4,2,48,384]{3,2,1,0:T(8,128)(2,1)S(1)}, u32[]{:S(2)}, u32[]{:S(2)}) collective-permute-start(bf16[4,2,48,384]{3,2,1,0:T(8,128)(2,1)S(1)} %pad_maximum_fusion.refs_0_), channel_id=1, source_target_pairs={{0,12},{4,0},{8,4},{12,8},{1,13},{5,1},{9,5},{13,9},{2,14},{6,2},{... | collective-permute-start | bytes 884744 | tf_op jit(solution)/shard_map/ppermute | solution.py:115
  70.3 12.6 %collective-permute-start.11 = (bf16[4,2,48,384]{3,2,1,0:T(8,128)(2,1)S(1)}, bf16[4,2,48,384]{3,2,1,0:T(8,128)(2,1)S(1)}, u32[]{:S(2)}, u32[]{:S(2)}) collective-permute-start(bf16[4,2,48,384]{3,2,1,0:T(8,128)(2,1)S(1)} %pad_maximum_fusion.1.refs_4_), channel_id=1, source_target_pairs={{0,16},{16,32},{32,48},{48,0},{1,17},{17,33},{33,49},{49,1},{2,18}... | collective-permute-start | bytes 884744 | tf_op jit(solution)/shard_map/ppermute | solution.py:115
  78.7 8.3 %collective-permute-start.12 = (bf16[4,2,48,384]{3,2,1,0:T(8,128)(2,1)S(1)}, bf16[4,2,48,384]{3,2,1,0:T(8,128)(2,1)}, u32[]{:S(2)}, u32[]{:S(2)}) collective-permute-start(bf16[4,2,48,384]{3,2,1,0:T(8,128)(2,1)S(1)} %pad_maximum_fusion.1.refs_4_), channel_id=1, source_target_pairs={{0,32},{16,48},{32,0},{48,16},{1,33},{17,49},{33,1},{49,17},{2,34}... | collective-permute-start | bytes 884744 | tf_op jit(solution)/shard_map/ppermute | solution.py:115
  78.7 8.3 %collective-permute-start.13 = (bf16[4,2,48,384]{3,2,1,0:T(8,128)(2,1)S(1)}, bf16[4,2,48,384]{3,2,1,0:T(8,128)(2,1)}, u32[]{:S(2)}, u32[]{:S(2)}) collective-permute-start(bf16[4,2,48,384]{3,2,1,0:T(8,128)(2,1)S(1)} %pad_maximum_fusion.1.refs_4_), channel_id=1, source_target_pairs={{0,48},{16,0},{32,16},{48,32},{1,49},{17,1},{33,17},{49,33},{2,50}... | collective-permute-start | bytes 884744 | tf_op jit(solution)/shard_map/ppermute | solution.py:115
  81.4 55.4 %collective-permute-start.28 = (bf16[2,16,48,768]{3,2,0,1:T(8,128)(2,1)}, bf16[2,16,48,768]{3,2,0,1:T(8,128)(2,1)}, u32[]{:S(2)}, u32[]{:S(2)}) collective-permute-start(bf16[2,16,48,768]{3,2,0,1:T(8,128)(2,1)} %bitcast.19), channel_id=1, source_target_pairs={{0,2},{2,0},{1,3},{3,1},{4,6},{6,4},{5,7},{7,5},{8,10},{10,8},{9,1... | collective-permute-start | bytes 7077896 | tf_op jit(solution)/shard_map/ppermute | solution.py:87
  81.6 7.9 %collective-permute-start.14 = (bf16[4,2,48,384]{3,2,1,0:T(8,128)(2,1)S(1)}, bf16[4,2,48,384]{3,2,1,0:T(8,128)(2,1)}, u32[]{:S(2)}, u32[]{:S(2)}) collective-permute-start(bf16[4,2,48,384]{3,2,1,0:T(8,128)(2,1)S(1)} %pad_maximum_fusion.refs_0_), channel_id=1, source_target_pairs={{0,2},{2,0},{1,3},{3,1},{4,6},{6,4},{5,7},{7,5},{8,10},{10,8},{9,1... | collective-permute-start | bytes 884744 | tf_op jit(solution)/shard_map/ppermute | solution.py:87
  82.9 6.5 %collective-permute-start.18 = (bf16[4,2,48,384]{3,2,1,0:T(8,128)(2,1)S(1)}, bf16[4,2,48,384]{3,2,1,0:T(8,128)(2,1)}, u32[]{:S(2)}, u32[]{:S(2)}) collective-permute-start(bf16[4,2,48,384]{3,2,1,0:T(8,128)(2,1)S(1)} %pad_maximum_fusion.1.refs_4_), channel_id=1, source_target_pairs={{0,2},{2,0},{1,3},{3,1},{4,6},{6,4},{5,7},{7,5},{8,10},{10,8},{9,1... | collective-permute-start | bytes 884744 | tf_op jit(solution)/shard_map/ppermute | solution.py:87
  87.0 2.9 collective-permute-start.15
  87.0 3.0 collective-permute-start.16
  89.4 8.0 %collective-permute-start.17 = (bf16[4,2,48,384]{3,2,1,0:T(8,128)(2,1)S(1)}, bf16[4,2,48,384]{3,2,1,0:T(8,128)(2,1)S(1)}, u32[]{:S(2)}, u32[]{:S(2)}) collective-permute-start(bf16[4,2,48,384]{3,2,1,0:T(8,128)(2,1)S(1)} %collective-permute-done.7.refs_3_), channel_id=1, source_target_pairs={{0,2},{2,0},{1,3},{3,1},{4,6},{6,4},{5,7},{7,5},{8,10},{10,8},{9,1... | collective-permute-start | bytes 884744 | tf_op jit(solution)/shard_map/ppermute | solution.py:87
  89.4 8.0 %collective-permute-start.19 = (bf16[4,2,48,384]{3,2,1,0:T(8,128)(2,1)S(1)}, bf16[4,2,48,384]{3,2,1,0:T(8,128)(2,1)S(1)}, u32[]{:S(2)}, u32[]{:S(2)}) collective-permute-start(bf16[4,2,48,384]{3,2,1,0:T(8,128)(2,1)S(1)} %collective-permute-done.11.refs_5_), channel_id=1, source_target_pairs={{0,2},{2,0},{1,3},{3,1},{4,6},{6,4},{5,7},{7,5},{8,10},{10,8},{9,1... | collective-permute-start | bytes 884744 | tf_op jit(solution)/shard_map/ppermute | solution.py:87
  89.9 7.5 %collective-permute-start.20 = (bf16[4,2,48,384]{3,2,1,0:T(8,128)(2,1)}, bf16[4,2,48,384]{3,2,1,0:T(8,128)(2,1)S(1)}, u32[]{:S(2)}, u32[]{:S(2)}) collective-permute-start(bf16[4,2,48,384]{3,2,1,0:T(8,128)(2,1)} %collective-permute-done.12.refs_6_), channel_id=1, source_target_pairs={{0,2},{2,0},{1,3},{3,1},{4,6},{6,4},{5,7},{7,5},{8,10},{10,8},{9,1... | collective-permute-start | bytes 884744 | tf_op jit(solution)/shard_map/ppermute | solution.py:87
  90.0 7.4 %collective-permute-start.21 = (bf16[4,2,48,384]{3,2,1,0:T(8,128)(2,1)}, bf16[4,2,48,384]{3,2,1,0:T(8,128)(2,1)S(1)}, u32[]{:S(2)}, u32[]{:S(2)}) collective-permute-start(bf16[4,2,48,384]{3,2,1,0:T(8,128)(2,1)} %collective-permute-done.13.refs_7_), channel_id=1, source_target_pairs={{0,2},{2,0},{1,3},{3,1},{4,6},{6,4},{5,7},{7,5},{8,10},{10,8},{9,1... | collective-permute-start | bytes 884744 | tf_op jit(solution)/shard_map/ppermute | solution.py:87
  105.5 21.8 %collective-permute-start.22 = (bf16[512,768]{1,0:T(8,128)(2,1)}, bf16[512,768]{1,0:T(8,128)(2,1)S(1)}, u32[]{:S(2)}, u32[]{:S(2)}) collective-permute-start(bf16[512,768]{1,0:T(8,128)(2,1)} %get-tuple-element.28), channel_id=1, source_target_pairs={{0,1},{1,0},{2,3},{3,2},{4,5},{5,4},{6,7},{7,6},{8,9},{9,8},{10,11... | collective-permute-start | bytes 2359304 | tf_op jit(solution)/shard_map/ppermute | solution.py:87
  112.3 14.9 %collective-permute-start.23 = (f32[2,768]{1,0:T(2,128)S(1)}, f32[2,768]{1,0:T(2,128)S(1)}, u32[]{:S(2)}, u32[]{:S(2)}) collective-permute-start(f32[2,768]{1,0:T(2,128)S(1)} %add.156), channel_id=1, source_target_pairs={{0,1},{1,0},{2,3},{3,2},{4,5},{5,4},{6,7},{7,6},{8,9},{9,8},{10,11... | collective-permute-start | bytes 18440 | tf_op jit(solution)/shard_map/ppermute | solution.py:87
  134.7 20.4 %collective-permute-start.29 = (bf16[512,768]{1,0:T(8,128)(2,1)}, bf16[512,768]{1,0:T(8,128)(2,1)S(1)}, u32[]{:S(2)}, u32[]{:S(2)}) collective-permute-start(bf16[512,768]{1,0:T(8,128)(2,1)} %get-tuple-element.31.refs_0_), channel_id=1, source_target_pairs={{0,1},{1,0},{2,3},{3,2},{4,5},{5,4},{6,7},{7,6},{8,9},{9,8},{10,11... | collective-permute-start | bytes 2359304 | tf_op jit(solution)/shard_map/ppermute | solution.py:87
  160.1 5.3 %collective-permute-start.30 = (f32[6,512]{1,0:T(8,128)S(1)}, f32[6,512]{1,0:T(8,128)S(1)}, u32[]{:S(2)}, u32[]{:S(2)}) collective-permute-start(f32[6,512]{1,0:T(8,128)S(1)} %stack.115), channel_id=1, source_target_pairs={{0,1},{1,0},{2,3},{3,2},{4,5},{5,4},{6,7},{7,6},{8,9},{9,8},{10,11... | collective-permute-start | bytes 36872 | tf_op jit(solution)/shard_map/ppermute | solution.py:87
  162.3 8.8 %collective-permute-start.35 = (bf16[512,768]{1,0:T(8,128)(2,1)}, bf16[512,768]{1,0:T(8,128)(2,1)}, u32[]{:S(2)}, u32[]{:S(2)}) collective-permute-start(bf16[512,768]{1,0:T(8,128)(2,1)} %get-tuple-element.31.refs_0_), channel_id=1, source_target_pairs={{0,2},{2,0},{1,3},{3,1},{4,6},{6,4},{5,7},{7,5},{8,10},{10,8},{9,1... | collective-permute-start | bytes 2359304 | tf_op jit(solution)/shard_map/ppermute | solution.py:87
  162.3 8.8 %collective-permute-start.36 = (bf16[512,768]{1,0:T(8,128)(2,1)}, bf16[512,768]{1,0:T(8,128)(2,1)}, u32[]{:S(2)}, u32[]{:S(2)}) collective-permute-start(bf16[512,768]{1,0:T(8,128)(2,1)} %copy-done.30), channel_id=1, source_target_pairs={{0,2},{2,0},{1,3},{3,1},{4,6},{6,4},{5,7},{7,5},{8,10},{10,8},{9,1... | collective-permute-start | bytes 2359304 | tf_op jit(solution)/shard_map/ppermute | solution.py:87
  179.4 64.1 %all-to-all-start.1 = ((bf16[16,2,48,768]{3,2,1,0:T(8,128)(2,1)}), bf16[16,2,48,768]{3,2,1,0:T(8,128)(2,1)}, u32[]{:S(2)}, u32[]{:S(2)}) async-start(bf16[16,2,48,768]{3,2,1,0:T(8,128)(2,1)} %shard_map.123), calls=%async_computation.1 | async-start | bytes 4718592 | tf_op jit(solution)/shard_map/all_to_all | solution.py:207
  188.7 21.2 %collective-permute-start.31 = (bf16[512,768]{1,0:T(8,128)(2,1)S(1)}, bf16[512,768]{1,0:T(8,128)(2,1)}, u32[]{:S(2)}, u32[]{:S(2)}) collective-permute-start(bf16[512,768]{1,0:T(8,128)(2,1)S(1)} %convolution_convert_fusion), channel_id=1, source_target_pairs={{0,1},{1,0},{2,3},{3,2},{4,5},{5,4},{6,7},{7,6},{8,9},{9,8},{10,11... | collective-permute-start | bytes 2359304 | tf_op jit(solution)/shard_map/ppermute | solution.py:87
  219.2 20.3 %collective-permute-start.32 = (bf16[512,768]{1,0:T(8,128)(2,1)}, bf16[512,768]{1,0:T(8,128)(2,1)}, u32[]{:S(2)}, u32[]{:S(2)}) collective-permute-start(bf16[512,768]{1,0:T(8,128)(2,1)} %get-tuple-element.33.refs_0_), channel_id=1, source_target_pairs={{0,1},{1,0},{2,3},{3,2},{4,5},{5,4},{6,7},{7,6},{8,9},{9,8},{10,11... | collective-permute-start | bytes 2359304 | tf_op jit(solution)/shard_map/ppermute | solution.py:87
  221.3 18.1 %collective-permute-start.34 = (bf16[512,768]{1,0:T(8,128)(2,1)}, bf16[512,768]{1,0:T(8,128)(2,1)}, u32[]{:S(2)}, u32[]{:S(2)}) collective-permute-start(bf16[512,768]{1,0:T(8,128)(2,1)} %get-tuple-element.25.refs_17_), channel_id=1, source_target_pairs={{0,2},{2,0},{1,3},{3,1},{4,6},{6,4},{5,7},{7,5},{8,10},{10,8},{9,1... | collective-permute-start | bytes 2359304 | tf_op jit(solution)/shard_map/ppermute | solution.py:87
  221.3 18.1 %collective-permute-start.33 = (bf16[512,768]{1,0:T(8,128)(2,1)}, bf16[512,768]{1,0:T(8,128)(2,1)}, u32[]{:S(2)}, u32[]{:S(2)}) collective-permute-start(bf16[512,768]{1,0:T(8,128)(2,1)} %get-tuple-element.33.refs_0_), channel_id=1, source_target_pairs={{0,2},{2,0},{1,3},{3,1},{4,6},{6,4},{5,7},{7,5},{8,10},{10,8},{9,1... | collective-permute-start | bytes 2359304 | tf_op jit(solution)/shard_map/ppermute | solution.py:87
  239.4 19.0 %collective-permute-start.38 = (bf16[512,768]{1,0:T(8,128)(2,1)}, bf16[512,768]{1,0:T(8,128)(2,1)}, u32[]{:S(2)}, u32[]{:S(2)}) collective-permute-start(bf16[512,768]{1,0:T(8,128)(2,1)} %collective-permute-done.32.refs_0_), channel_id=1, source_target_pairs={{0,2},{2,0},{1,3},{3,1},{4,6},{6,4},{5,7},{7,5},{8,10},{10,8},{9,1... | collective-permute-start | bytes 2359304 | tf_op jit(solution)/shard_map/ppermute | solution.py:87
  243.5 26.7 %all-to-all-start.2 = ((bf16[16,1,48,768]{3,2,1,0:T(8,128)(2,1)}), bf16[16,1,48,768]{3,2,1,0:T(8,128)(2,1)}, u32[]{:S(2)}, u32[]{:S(2)}) async-start(bf16[16,1,48,768]{3,2,1,0:T(8,128)(2,1)} %shard_map.122), calls=%async_computation.2 | async-start | bytes 2359296 | tf_op jit(solution)/shard_map/all_to_all | solution.py:207
  270.3 22.6 %all-to-all-start.3 = ((bf16[16,1,48,768]{3,2,1,0:T(8,128)(2,1)}), bf16[16,1,48,768]{3,2,1,0:T(8,128)(2,1)}, u32[]{:S(2)}, u32[]{:S(2)}) async-start(bf16[16,1,48,768]{3,2,1,0:T(8,128)(2,1)} %shard_map.124), calls=%async_computation.3 | async-start | bytes 2359296 | tf_op jit(solution)/shard_map/all_to_all | solution.py:207
  275.6 7.3 %collective-permute-start.43 = (f32[24,768]{1,0:T(8,128)S(1)}, f32[24,768]{1,0:T(8,128)S(1)}, u32[]{:S(2)}, u32[]{:S(2)}) collective-permute-start(f32[24,768]{1,0:T(8,128)S(1)} %get-tuple-element.64), channel_id=1, source_target_pairs={{0,64},{64,0},{1,65},{65,1},{2,66},{66,2},{3,67},{67,3},{4,68},{68... | collective-permute-start | bytes 221192 | tf_op jit(solution)/shard_map/ppermute | solution.py:87
  275.8 7.1 %collective-permute-start.44 = (f32[24,768]{1,0:T(8,128)S(1)}, f32[24,768]{1,0:T(8,128)S(1)}, u32[]{:S(2)}, u32[]{:S(2)}) collective-permute-start(f32[24,768]{1,0:T(8,128)S(1)} %get-tuple-element.63), channel_id=1, source_target_pairs={{0,66},{2,64},{64,2},{66,0},{1,67},{3,65},{65,3},{67,1},{4,70},{6,... | collective-permute-start | bytes 221192 | tf_op jit(solution)/shard_map/ppermute | solution.py:221
  275.8 7.1 %collective-permute-start.45 = (f32[24,768]{1,0:T(8,128)S(1)}, f32[24,768]{1,0:T(8,128)S(1)}, u32[]{:S(2)}, u32[]{:S(2)}) collective-permute-start(f32[24,768]{1,0:T(8,128)S(1)} %select_bitcast_fusion), channel_id=1, source_target_pairs={{0,2},{2,0},{1,3},{3,1},{4,6},{6,4},{5,7},{7,5},{8,10},{10,8},{9,1... | collective-permute-start | bytes 221192 | tf_op jit(solution)/shard_map/ppermute | solution.py:87
  295.4 4.4 %collective-permute-start.39 = (f32[24,768]{1,0:T(8,128)S(1)}, f32[24,768]{1,0:T(8,128)S(1)}, u32[]{:S(2)}, u32[]{:S(2)}) collective-permute-start(f32[24,768]{1,0:T(8,128)S(1)} %get-tuple-element.68), channel_id=1, source_target_pairs={{0,64},{64,0},{1,65},{65,1},{2,66},{66,2},{3,67},{67,3},{4,68},{68... | collective-permute-start | bytes 221192 | tf_op jit(solution)/shard_map/ppermute | solution.py:87
  295.8 9.5 %collective-permute-start.46 = (f32[24]{0:T(128)S(1)}, f32[24]{0:T(128)S(1)}, u32[]{:S(2)}, u32[]{:S(2)}) collective-permute-start(f32[24]{0:T(128)S(1)} %multiply_reduce_fusion.3), channel_id=1, source_target_pairs={{0,1},{1,0},{2,3},{3,2},{4,5},{5,4},{6,7},{7,6},{8,9},{9,8},{10,11... | collective-permute-start | bytes 296 | tf_op jit(solution)/shard_map/ppermute | solution.py:87
  299.3 6.0 %collective-permute-start.40 = (f32[24,768]{1,0:T(8,128)S(1)}, f32[24,768]{1,0:T(8,128)S(1)}, u32[]{:S(2)}, u32[]{:S(2)}) collective-permute-start(f32[24,768]{1,0:T(8,128)S(1)} %get-tuple-element.67), channel_id=1, source_target_pairs={{0,66},{2,64},{64,2},{66,0},{1,67},{3,65},{65,3},{67,1},{4,70},{6,... | collective-permute-start | bytes 221192 | tf_op jit(solution)/shard_map/ppermute | solution.py:221
  299.9 5.4 %collective-permute-start.41 = (f32[24,768]{1,0:T(8,128)S(1)}, f32[24,768]{1,0:T(8,128)S(1)}, u32[]{:S(2)}, u32[]{:S(2)}) collective-permute-start(f32[24,768]{1,0:T(8,128)S(1)} %get-tuple-element.65), channel_id=1, source_target_pairs={{0,2},{2,0},{1,3},{3,1},{4,6},{6,4},{5,7},{7,5},{8,10},{10,8},{9,1... | collective-permute-start | bytes 221192 | tf_op jit(solution)/shard_map/ppermute | solution.py:87
  305.5 5.1 %collective-permute-start.42 = (f32[24]{0:T(128)S(1)}, f32[24]{0:T(128)S(1)}, u32[]{:S(2)}, u32[]{:S(2)}) collective-permute-start(f32[24]{0:T(128)S(1)} %multiply_reduce_fusion.4), channel_id=1, source_target_pairs={{0,1},{1,0},{2,3},{3,2},{4,5},{5,4},{6,7},{7,6},{8,9},{9,8},{10,11... | collective-permute-start | bytes 296 | tf_op jit(solution)/shard_map/ppermute | solution.py:87
  (35 other events, 331.7 us)

commit v2 on v1

--- a/solution.py
+++ b/solution.py
@@ -33,32 +33,44 @@
     return jnp.dot(left, right, preferred_element_type=F32)
 
 
+def causal_halves(length):
+    half = length // 2
+    return ((0, half), (half, length))
+
+
 def probs_kernel(q_ref, k_ref, p_ref):
-    length = q_ref.shape[0]
-    scores = contract_last(q_ref[...], k_ref[...]) * (HS**-0.5)
-    row_pos = lax.broadcasted_iota(jnp.int32, (length, length), 0)
-    col_pos = lax.broadcasted_iota(jnp.int32, (length, length), 1)
-    scores = jnp.where(row_pos >= col_pos, scores, -1e30)
-    terms = jnp.exp(scores - jnp.max(scores, axis=1, keepdims=True))
-    p_ref[0] = terms * (1.0 / jnp.sum(terms, axis=1, keepdims=True))
+    for lo, hi in causal_halves(q_ref.shape[0]):
+        scores = contract_last(q_ref[lo:hi, :], k_ref[:hi, :]) * (HS**-0.5)
+        row_pos = lax.broadcasted_iota(jnp.int32, scores.shape, 0) + lo
+        col_pos = lax.broadcasted_iota(jnp.int32, scores.shape, 1)
+        scores = jnp.where(row_pos >= col_pos, scores, -1e30)
+        terms = jnp.exp(scores - jnp.max(scores, axis=1, keepdims=True))
+        p_ref[0, lo:hi, :hi] = terms * (1.0 / jnp.sum(terms, axis=1, keepdims=True))
 
 
 def forward_kernel(p_ref, own_ref, peer_ref, rate_ref, v_ref, attn_ref):
     value = ((own_ref[...] + peer_ref[...].astype(F32)) * rate_ref[0:1, :]).astype(BF16)
     v_ref[...] = value
-    attn_ref[...] = matmul(p_ref[0].astype(BF16), value).astype(BF16)
+    for lo, hi in causal_halves(p_ref.shape[1]):
+        attn_ref[lo:hi, :] = matmul(p_ref[0, lo:hi, :hi].astype(BF16), value[:hi]).astype(BF16)
 
 
 def backward_kernel(q_ref, k_ref, v_ref, p_ref, own_ref, peer_ref, dq_ref, dk_ref, dv_ref):
     scale = HS**-0.5
-    prob = p_ref[0]
     grad = (own_ref[...] + peer_ref[...].astype(F32)).astype(BF16)
-    grad_prob = contract_last(grad, v_ref[...])
-    delta = jnp.sum(prob * grad_prob, axis=1, keepdims=True)
-    grad_score = (prob * (grad_prob - delta)).astype(BF16)
-    dv_ref[...] = contract_first(prob.astype(BF16), grad).astype(BF16)
-    dq_ref[...] = (matmul(grad_score, k_ref[...]) * scale).astype(BF16)
-    dk_ref[...] = (contract_first(grad_score, q_ref[...]) * scale).astype(BF16)
+    grad_keys, grad_values = [], []
+    for lo, hi in causal_halves(p_ref.shape[1]):
+        prob = p_ref[0, lo:hi, :hi]
+        grad_prob = contract_last(grad[lo:hi], v_ref[:hi, :])
+        delta = jnp.sum(prob * grad_prob, axis=1, keepdims=True)
+        grad_score = (prob * (grad_prob - delta)).astype(BF16)
+        dq_ref[lo:hi, :] = (matmul(grad_score, k_ref[:hi, :]) * scale).astype(BF16)
+        grad_keys.append(contract_first(grad_score, q_ref[lo:hi, :]))
+        grad_values.append(contract_first(prob.astype(BF16), grad[lo:hi]))
+    half = grad_keys[0].shape[0]
+    for out_ref, (early, late), rate in ((dk_ref, grad_keys, scale), (dv_ref, grad_values, 1.0)):
+        out_ref[:half, :] = ((early + late[:half]) * rate).astype(BF16)
+        out_ref[half:, :] = (late[half:] * rate).astype(BF16)
 
 
 def heads_call(kernel, heads, operands, results, dots):

time: 315 us -> 315 us (level)
  no operation moved by 1% of the time
where the time goes in v2:
time: 315 us; the launch traced here: 312 us
  waiting for transfers between devices  118 us (37%)
  starting transfers between devices  79.2 us (25%)
  Pallas kernels  43.2 us (14%)
  other arithmetic  42.4 us (13%)
  matrix products  19.9 us (6%)
  local copies, waits for them, and re-layouts  7.37 us (2%)
    ppermute x31, waiting for transfers between devices, exchanged(): return lax.ppermute(value, axis, SWAP)  70.6 us
    ppermute x12, waiting for transfers between devices, shifted(): lax.ppermute(value, axis, [(i, (i + step) % count) for i in range(count)])  32.4 us
    ppermute x12, starting transfers between devices, shifted(): lax.ppermute(value, axis, [(i, (i + step) % count) for i in range(count)])  25.5 us
    ppermute x31, starting transfers between devices, exchanged(): return lax.ppermute(value, axis, SWAP)  25.4 us
    pallas_call x3, Pallas kernels, heads_call(): pl.pallas_call(kernel, grid=(heads,), in_specs=[spec(o.shape, first) for...  22.7 us
    all_to_all x3, starting transfers between devices, arriving(): return lax.all_to_all(tiles, YZ, 0, 0, tiled=True)  16.6 us
    pallas_call x3, Pallas kernels, products(): pl.pallas_call(product_kernel, grid=(steps,), in_specs=[pl.BlockSpec((tok...  14.1 us
    all_to_all x3, waiting for transfers between devices, arriving(): return lax.all_to_all(tiles, YZ, 0, 0, tiled=True)  12.3 us
  transfers between devices with their start and end apart: 51, of which 20 were waited for; matrix products, arithmetic and copies ran while one was open for 18% of the time, Pallas kernels for 12%

profile of v2, /device:TPU:6, one launch (start us, length us, event | category | flops | bytes accessed | tf_op | source)
XLA Modules:
  0.0 311.6 jit_solution(13026881074042002203)
XLA Ops:
  4.8 2.2 collective-permute-start.24
  7.0 3.0 collective-permute-done.24
  14.2 8.2 %all-to-all-start = ((bf16[16,2,48,768]{3,2,1,0:T(8,128)(2,1)}), bf16[16,2,48,768]{3,2,1,0:T(8,128)(2,1)}, u32[]{:S(2)}, u32[]{:S(2)}) async-start(bf16[16,2,48,768]{3,2,1,0:T(8,128)(2,1)} %broadcast_in_dim.8), calls=%async_computation | async-start | bytes 4718592 | tf_op jit(solution)/shard_map/all_to_all | solution.py:121
  22.6 4.3 %collective-permute-done = bf16[24,1536]{1,0:T(8,128)(2,1)S(1)} collective-permute-done((bf16[24,1536]{1,0:T(8,128)(2,1)S(1)}, bf16[24,1536]{1,0:T(8,128)(2,1)S(1)}, u32[]{:S(2)}, u32[]{:S(2)}) %collective-permute-start) | collective-permute-done | bytes 73760 | tf_op jit(solution)/shard_map/ppermute | solution.py:99
  28.4 3.2 %collective-permute-start.4 = (bf16[2,48,384]{2,1,0:T(8,128)(2,1)S(1)}, bf16[2,48,384]{2,1,0:T(8,128)(2,1)S(1)}, u32[]{:S(2)}, u32[]{:S(2)}) collective-permute-start(bf16[2,48,384]{2,1,0:T(8,128)(2,1)S(1)} %get-tuple-element.74), channel_id=1, source_target_pairs={{0,48},{16,0},{32,16},{48,32},{1,49},{17,1},{33,17},{49,33},{2,50}... | collective-permute-start | bytes 221192 | tf_op jit(solution)/shard_map/ppermute | solution.py:127
  33.2 20.0 %collective-permute-done.4 = bf16[2,48,384]{2,1,0:T(8,128)(2,1)S(1)} collective-permute-done((bf16[2,48,384]{2,1,0:T(8,128)(2,1)S(1)}, bf16[2,48,384]{2,1,0:T(8,128)(2,1)S(1)}, u32[]{:S(2)}, u32[]{:S(2)}) %collective-permute-start.4) | collective-permute-done | bytes 73760 | tf_op jit(solution)/shard_map/ppermute | solution.py:127
  53.2 2.9 collective-permute-done.3
  61.1 2.8 collective-permute-start.6
  65.7 3.5 %collective-permute-done.9 = bf16[2,48,384]{2,1,0:T(8,128)(2,1)S(1)} collective-permute-done((bf16[2,48,384]{2,1,0:T(8,128)(2,1)S(1)}, bf16[2,48,384]{2,1,0:T(8,128)(2,1)S(1)}, u32[]{:S(2)}, u32[]{:S(2)}) %collective-permute-start.9) | collective-permute-done | bytes 73760 | tf_op jit(solution)/shard_map/ppermute | solution.py:127
  70.3 8.4 %collective-permute-start.11 = (bf16[4,2,48,384]{3,2,1,0:T(8,128)(2,1)S(1)}, bf16[4,2,48,384]{3,2,1,0:T(8,128)(2,1)S(1)}, u32[]{:S(2)}, u32[]{:S(2)}) collective-permute-start(bf16[4,2,48,384]{3,2,1,0:T(8,128)(2,1)S(1)} %pad_maximum_fusion.1.refs_4_), channel_id=1, source_target_pairs={{0,16},{16,32},{32,48},{48,0},{1,17},{17,33},{33,49},{49,1},{2,18}... | collective-permute-start | bytes 884744 | tf_op jit(solution)/shard_map/ppermute | solution.py:127
  78.7 2.8 collective-permute-start.13
  82.9 4.1 %collective-permute-done.12.refs_6_ = bf16[4,2,48,384]{3,2,1,0:T(8,128)(2,1)} collective-permute-done((bf16[4,2,48,384]{3,2,1,0:T(8,128)(2,1)S(1)}, bf16[4,2,48,384]{3,2,1,0:T(8,128)(2,1)}, u32[]{:S(2)}, u32[]{:S(2)}) %collective-permute-start.12) | collective-permute-done | bytes 294944 | tf_op jit(solution)/shard_map/ppermute | solution.py:127
  90.5 6.8 %shard_map.118.p_ref = f32[6,512,512]{2,1,0:T(8,128)} custom-call(bf16[512,768]{1,0:T(8,128)(2,1)} %q_ref.3, bf16[512,768]{1,0:T(8,128)(2,1)} %k_ref.3), custom_call_target="tpu_custom_call" | custom-call | flops 805306368 | bytes 10223616 | tf_op jit(solution)/shard_map/pallas_call | solution.py:83
  98.9 6.5 %shard_map.119 = (bf16[2,768,768]{2,1,0:T(8,128)(2,1)}, bf16[2,768,768]{2,1,0:T(8,128)(2,1)}, bf16[512,768]{1,0:T(8,128)(2,1)}) custom-call(s32[2]{0:T(128)} %pad_add_fusion.place_ref, bf16[4,2,48,384]{3,2,1,0:T(8,128)(2,1)} %copy-done.14, bf16[4,2,48,384]{3,2,1,0:T(8,128)(2,1)} %copy-done.20, bf16[4,2,48,384]{3,2,1,0:T(8,128)(2,1)} %copy-done.21, ...), custom_call_target="tpu_custom_call" | custom-call | flops 1207959552 | bytes 4718592 | tf_op jit(solution)/shard_map/pallas_call | solution.py:175
  105.4 2.4 collective-permute-start.22
  107.8 3.5 %multiply_reduce_fusion = (f32[2,768]{1,0:T(2,128)S(1)}, f32[2,768]{1,0:T(2,128)S(1)}) fusion(bf16[2,768,768]{2,1,0:T(8,128)(2,1)} %get-tuple-element.30, bf16[2,768,768]{2,1,0:T(8,128)(2,1)} %get-tuple-element.29), kind=kLoop, calls=%fused_computation.14 | loop fusion | flops 7074816 | bytes 4730880 | tf_op jit(solution)/shard_map/reduce_sum | solution.py:290
  115.7 11.4 %collective-permute-done.23 = f32[2,768]{1,0:T(2,128)S(1)} collective-permute-done((f32[2,768]{1,0:T(2,128)S(1)}, f32[2,768]{1,0:T(2,128)S(1)}, u32[]{:S(2)}, u32[]{:S(2)}) %collective-permute-start.23) | collective-permute-done | bytes 6176 | tf_op jit(solution)/shard_map/ppermute | solution.py:99
  128.2 6.3 %shard_map.120 = (bf16[512,768]{1,0:T(8,128)(2,1)}, bf16[512,768]{1,0:T(8,128)(2,1)}) custom-call(f32[6,512,512]{2,1,0:T(8,128)} %shard_map.118.p_ref, f32[512,768]{1,0:T(8,128)} %convolution_add_fusion.own_ref, bf16[512,768]{1,0:T(8,128)(2,1)} %copy-done.18, f32[8,768]{1,0:T(8,128)} %broadcast_in_dim.7.rate_ref), custom_call_target="tpu_custom_call" | custom-call | flops 805306368 | bytes 10223616 | tf_op jit(solution)/shard_map/pallas_call | solution.py:83
  136.7 4.9 %maximum_select_fusion = bf16[2,16,48,1536]{3,2,0,1:T(8,128)(2,1)S(1)} fusion(bf16[2,16,48,768]{3,2,0,1:T(8,128)(2,1)} %collective-permute-done.28, bf16[2,16,48,768]{3,2,0,1:T(8,128)(2,1)} %bitcast.19, pred[]{:T(512)S(6)} %eq.6), kind=kLoop, calls=%fused_computation.11 | loop fusion | flops 21233664 | bytes 9437185 | tf_op jit(solution)/shard_map/jit(_where)/select_n | solution.py:112
  144.1 10.8 %collective-permute-done.29.refs_2_ = bf16[512,768]{1,0:T(8,128)(2,1)S(1)} collective-permute-done((bf16[512,768]{1,0:T(8,128)(2,1)}, bf16[512,768]{1,0:T(8,128)(2,1)S(1)}, u32[]{:S(2)}, u32[]{:S(2)}) %collective-permute-start.29) | collective-permute-done | bytes 786464 | tf_op jit(solution)/shard_map/ppermute | solution.py:99
  157.1 2.8 fusion.2
  159.9 2.2 collective-permute-start.30
  162.6 2.6 collective-permute-done.30
  165.3 3.5 %multiply_convert_fusion = bf16[512,1536]{1,0:T(8,128)(2,1)S(1)} fusion(f32[512,1536]{1,0:T(8,128)S(1)} %get-tuple-element.48, bf16[512,1536]{1,0:T(8,128)(2,1)} %param.13, f32[512]{0:T(512)S(1)} %get-tuple-element.87, f32[512]{0:T(512)S(1)} %get-tuple-element.91, f32[512]{0:T(512)S(1)} %get-tuple-element.88, f32[512]{0:T(512)S(1)} %bitcast.84, ...), kind=kLoop, calls=%fused_computation.27 | loop fusion | flops 13369344 | bytes 7878656 | tf_op jit(solution)/shard_map/convert_element_type | solution.py:338
  170.9 2.4 collective-permute-done.37.refs_5_
  173.4 5.9 %shard_map.123 = bf16[16,2,48,768]{3,2,1,0:T(8,128)(2,1)} custom-call(bf16[512,768]{1,0:T(8,128)(2,1)} %get-tuple-element.31.refs_0_, bf16[512,768]{1,0:T(8,128)(2,1)} %collective-permute-done.35.refs_1_, bf16[512,768]{1,0:T(8,128)(2,1)} %copy-done.30, bf16[512,768]{1,0:T(8,128)(2,1)} %collective-permute-done.36.refs_3_, ...), custom_call_target="tpu_custom_call" | custom-call | flops 2415919104 | bytes 2359296 | tf_op jit(solution)/shard_map/pallas_call | solution.py:200
  179.3 5.5 %all-to-all-start.1 = ((bf16[16,2,48,768]{3,2,1,0:T(8,128)(2,1)}), bf16[16,2,48,768]{3,2,1,0:T(8,128)(2,1)}, u32[]{:S(2)}, u32[]{:S(2)}) async-start(bf16[16,2,48,768]{3,2,1,0:T(8,128)(2,1)} %shard_map.123), calls=%async_computation.1 | async-start | bytes 4718592 | tf_op jit(solution)/shard_map/all_to_all | solution.py:219
  184.8 3.7 %convolution_convert_fusion = bf16[512,768]{1,0:T(8,128)(2,1)S(1)} fusion(bf16[512,1536]{1,0:T(8,128)(2,1)} %copy-done.7, bf16[768,1536]{1,0:T(8,128)(2,1)} %bitcast.76), kind=kOutput, calls=%fused_computation.36 | convolution fusion | flops 1208352768 | bytes 4718592 | tf_op jit(solution)/shard_map/dot_general | solution.py:25
  188.5 2.4 collective-permute-start.31
  191.0 2.6 fusion.39.own_ref
  193.5 16.2 %collective-permute-done.31.peer_ref = bf16[512,768]{1,0:T(8,128)(2,1)} collective-permute-done((bf16[512,768]{1,0:T(8,128)(2,1)S(1)}, bf16[512,768]{1,0:T(8,128)(2,1)}, u32[]{:S(2)}, u32[]{:S(2)}) %collective-permute-start.31) | collective-permute-done | bytes 786464 | tf_op jit(solution)/shard_map/ppermute | solution.py:99
  209.7 9.5 %shard_map.121 = (bf16[512,768]{1,0:T(8,128)(2,1)}, bf16[512,768]{1,0:T(8,128)(2,1)}, bf16[512,768]{1,0:T(8,128)(2,1)}) custom-call(bf16[512,768]{1,0:T(8,128)(2,1)} %q_ref.3, bf16[512,768]{1,0:T(8,128)(2,1)} %k_ref.3, bf16[512,768]{1,0:T(8,128)(2,1)} %get-tuple-element.32.v_ref, f32[6,512,512]{2,1,0:T(8,128)} %shard_map.118.p_ref, ...), custom_call_target="tpu_custom_call" | custom-call | flops 3221225472 | bytes 10223616 | tf_op jit(solution)/shard_map/pallas_call | solution.py:83
  219.3 2.1 collective-permute-start.32
  221.9 17.6 %collective-permute-done.32.refs_0_ = bf16[512,768]{1,0:T(8,128)(2,1)} collective-permute-done((bf16[512,768]{1,0:T(8,128)(2,1)}, bf16[512,768]{1,0:T(8,128)(2,1)}, u32[]{:S(2)}, u32[]{:S(2)}) %collective-permute-start.32) | collective-permute-done | bytes 786464 | tf_op jit(solution)/shard_map/ppermute | solution.py:99
  239.5 4.1 %shard_map.122 = bf16[16,1,48,768]{3,2,1,0:T(8,128)(2,1)} custom-call(bf16[512,768]{1,0:T(8,128)(2,1)} %get-tuple-element.33.refs_0_, bf16[512,768]{1,0:T(8,128)(2,1)} %collective-permute-done.33.refs_1_, bf16[512,768]{1,0:T(8,128)(2,1)} %get-tuple-element.24.refs_16_.refs_2_, bf16[512,768]{1,0:T(8,128)(2,1)} %collective-permute-done.34.refs_3_), custom_call_target="tpu_custom_call" | custom-call | flops 1207959552 | bytes 2359296 | tf_op jit(solution)/shard_map/pallas_call | solution.py:200
  243.6 6.7 %all-to-all-start.2 = ((bf16[16,1,48,768]{3,2,1,0:T(8,128)(2,1)}), bf16[16,1,48,768]{3,2,1,0:T(8,128)(2,1)}, u32[]{:S(2)}, u32[]{:S(2)}) async-start(bf16[16,1,48,768]{3,2,1,0:T(8,128)(2,1)} %shard_map.122), calls=%async_computation.2 | async-start | bytes 2359296 | tf_op jit(solution)/shard_map/all_to_all | solution.py:219
  250.3 5.0 %divide_convert_fusion = bf16[2,768,1536]{2,1,0:T(8,128)(2,1)S(1)} fusion(bf16[2,768,768]{2,1,0:T(8,128)(2,1)} %get-tuple-element.30, bf16[2,768,768]{2,1,0:T(8,128)(2,1)} %get-tuple-element.29, f32[2,768]{1,0:T(2,128)S(1)} %get-tuple-element.46, pred[]{:T(512)S(6)} %eq.6), kind=kLoop, calls=%fused_computation | loop fusion | flops 28311552 | bytes 9443329 | tf_op jit(solution)/shard_map/convert.1
  255.4 3.1 %fusion.11 = f32[512,1536]{1,0:T(8,128)} fusion(bf16[512,768]{1,0:T(8,128)(2,1)S(1)} %copy-done.31, bf16[2,768,1536]{2,1,0:T(8,128)(2,1)S(1)} %divide_convert_fusion), kind=kOutput, calls=%fused_computation.32 | convolution fusion | flops 1207959552 | bytes 6291456 | tf_op jit(solution)/shard_map/dot_general | solution.py:33
  258.5 4.1 %shard_map.124 = bf16[16,1,48,768]{3,2,1,0:T(8,128)(2,1)} custom-call(bf16[512,768]{1,0:T(8,128)(2,1)} %collective-permute-done.32.refs_0_, bf16[512,768]{1,0:T(8,128)(2,1)} %collective-permute-done.38.refs_1_, bf16[512,768]{1,0:T(8,128)(2,1)} %get-tuple-element.24.refs_16_.refs_2_, bf16[512,768]{1,0:T(8,128)(2,1)} %collective-permute-done.34.refs_3_), custom_call_target="tpu_custom_call" | custom-call | flops 1207959552 | bytes 2359296 | tf_op jit(solution)/shard_map/pallas_call | solution.py:200
  265.3 5.1 %all-to-all-done.2 = bf16[16,1,48,768]{3,2,1,0:T(8,128)(2,1)} async-done(((bf16[16,1,48,768]{3,2,1,0:T(8,128)(2,1)}), bf16[16,1,48,768]{3,2,1,0:T(8,128)(2,1)}, u32[]{:S(2)}, u32[]{:S(2)}) %all-to-all-start.2) | async-done | bytes 1179680 | tf_op jit(solution)/shard_map/all_to_all | solution.py:219
  270.4 4.4 %all-to-all-start.3 = ((bf16[16,1,48,768]{3,2,1,0:T(8,128)(2,1)}), bf16[16,1,48,768]{3,2,1,0:T(8,128)(2,1)}, u32[]{:S(2)}, u32[]{:S(2)}) async-start(bf16[16,1,48,768]{3,2,1,0:T(8,128)(2,1)} %shard_map.124), calls=%async_computation.3 | async-start | bytes 2359296 | tf_op jit(solution)/shard_map/all_to_all | solution.py:219
  278.0 5.0 %fusion.10 = f32[512,1536]{1,0:T(8,128)} fusion(bf16[512,768]{1,0:T(8,128)(2,1)} %collective-permute-done.32.refs_0_, bf16[2,768,1536]{2,1,0:T(8,128)(2,1)} %copy-done.9), kind=kOutput, calls=%fused_computation.30 | convolution fusion | flops 1207959552 | bytes 6291456 | tf_op jit(solution)/shard_map/dot_general | solution.py:33
  283.7 2.1 convert_reduce_fusion.2
  285.8 7.2 %all-to-all-done.3 = bf16[16,1,48,768]{3,2,1,0:T(8,128)(2,1)} async-done(((bf16[16,1,48,768]{3,2,1,0:T(8,128)(2,1)}), bf16[16,1,48,768]{3,2,1,0:T(8,128)(2,1)}, u32[]{:S(2)}, u32[]{:S(2)}) %all-to-all-start.3) | async-done | bytes 1179680 | tf_op jit(solution)/shard_map/all_to_all | solution.py:219
  295.8 3.6 %collective-permute-start.46 = (f32[24]{0:T(128)S(1)}, f32[24]{0:T(128)S(1)}, u32[]{:S(2)}, u32[]{:S(2)}) collective-permute-start(f32[24]{0:T(128)S(1)} %multiply_reduce_fusion.3), channel_id=1, source_target_pairs={{0,1},{1,0},{2,3},{3,2},{4,5},{5,4},{6,7},{7,6},{8,9},{9,8},{10,11... | collective-permute-start | bytes 296 | tf_op jit(solution)/shard_map/ppermute | solution.py:99
  300.1 5.3 %add_convert_fusion = (bf16[512,1536]{1,0:T(8,128)(2,1)}, bf16[512,1536]{1,0:T(8,128)(2,1)}) fusion(f32[512,1536]{1,0:T(8,128)} %fusion.10, f32[512,1536]{1,0:T(8,128)} %fusion.11, bf16[512,1536]{1,0:T(8,128)(2,1)} %param.13, f32[512]{0:T(512)S(1)} %get-tuple-element.91, f32[512]{0:T(512)S(1)} %get-tuple-element.88, f32[1536]{0:T(1024)S(1)} %get-tuple-element.89, ...), kind=kLoop, calls=%fused_computation.26 | loop fusion | flops 12582912 | bytes 15747072 | tf_op jit(solution)/shard_map/convert_element_type | solution.py:368
  305.6 2.2 collective-permute-start.42
  308.6 2.1 collective-permute-done.42
  (188 shorter events, 53.1 us)
Async XLA Ops:
  0.6 9.4 %collective-permute-start.25 = (bf16[24,1536]{1,0:T(8,128)(2,1)}, bf16[24,1536]{1,0:T(8,128)(2,1)S(1)}, u32[]{:S(2)}, u32[]{:S(2)}) collective-permute-start(bf16[24,1536]{1,0:T(8,128)(2,1)} %param.11), channel_id=1, source_target_pairs={{0,64},{64,0},{1,65},{65,1},{2,66},{66,2},{3,67},{67,3},{4,68},{68... | collective-permute-start | bytes 221192 | tf_op jit(solution)/shard_map/ppermute | solution.py:99
  2.6 7.6 %collective-permute-start.26 = (f32[24]{0:T(128)S(1)}, f32[24]{0:T(128)S(1)}, u32[]{:S(2)}, u32[]{:S(2)}) collective-permute-start(f32[24]{0:T(128)S(1)} %fusion.17), channel_id=1, source_target_pairs={{0,65},{1,64},{64,1},{65,0},{2,67},{3,66},{66,3},{67,2},{4,69},{5,... | collective-permute-start | bytes 296 | tf_op jit(solution)/shard_map/ppermute | solution.py:266
  4.8 5.2 %collective-permute-start.24 = (f32[2,24]{1,0:T(2,128)S(1)}, f32[2,24]{1,0:T(2,128)S(1)}, u32[]{:S(2)}, u32[]{:S(2)}) collective-permute-start(f32[2,24]{1,0:T(2,128)S(1)} %pad_maximum_fusion.4), channel_id=1, source_target_pairs={{0,1},{1,0},{2,3},{3,2},{4,5},{5,4},{6,7},{7,6},{8,9},{9,8},{10,11... | collective-permute-start | bytes 584 | tf_op jit(solution)/shard_map/ppermute | solution.py:265
  14.2 67.2 %all-to-all-start = ((bf16[16,2,48,768]{3,2,1,0:T(8,128)(2,1)}), bf16[16,2,48,768]{3,2,1,0:T(8,128)(2,1)}, u32[]{:S(2)}, u32[]{:S(2)}) async-start(bf16[16,2,48,768]{3,2,1,0:T(8,128)(2,1)} %broadcast_in_dim.8), calls=%async_computation | async-start | bytes 4718592 | tf_op jit(solution)/shard_map/all_to_all | solution.py:121
  22.4 4.4 %collective-permute-start = (bf16[24,1536]{1,0:T(8,128)(2,1)S(1)}, bf16[24,1536]{1,0:T(8,128)(2,1)S(1)}, u32[]{:S(2)}, u32[]{:S(2)}) collective-permute-start(bf16[24,1536]{1,0:T(8,128)(2,1)S(1)} %copy-done.17), channel_id=1, source_target_pairs={{0,64},{64,0},{1,65},{65,1},{2,66},{66,2},{3,67},{67,3},{4,68},{68... | collective-permute-start | bytes 221192 | tf_op jit(solution)/shard_map/ppermute | solution.py:99
  28.4 24.9 %collective-permute-start.4 = (bf16[2,48,384]{2,1,0:T(8,128)(2,1)S(1)}, bf16[2,48,384]{2,1,0:T(8,128)(2,1)S(1)}, u32[]{:S(2)}, u32[]{:S(2)}) collective-permute-start(bf16[2,48,384]{2,1,0:T(8,128)(2,1)S(1)} %get-tuple-element.74), channel_id=1, source_target_pairs={{0,48},{16,0},{32,16},{48,32},{1,49},{17,1},{33,17},{49,33},{2,50}... | collective-permute-start | bytes 221192 | tf_op jit(solution)/shard_map/ppermute | solution.py:127
  31.5 24.6 %collective-permute-start.3 = (bf16[2,48,384]{2,1,0:T(8,128)(2,1)S(1)}, bf16[2,48,384]{2,1,0:T(8,128)(2,1)S(1)}, u32[]{:S(2)}, u32[]{:S(2)}) collective-permute-start(bf16[2,48,384]{2,1,0:T(8,128)(2,1)S(1)} %get-tuple-element.74), channel_id=1, source_target_pairs={{0,32},{16,48},{32,0},{48,16},{1,33},{17,49},{33,1},{49,17},{2,34}... | collective-permute-start | bytes 221192 | tf_op jit(solution)/shard_map/ppermute | solution.py:127
  32.4 23.8 %collective-permute-start.2 = (bf16[2,48,384]{2,1,0:T(8,128)(2,1)S(1)}, bf16[2,48,384]{2,1,0:T(8,128)(2,1)S(1)}, u32[]{:S(2)}, u32[]{:S(2)}) collective-permute-start(bf16[2,48,384]{2,1,0:T(8,128)(2,1)S(1)} %get-tuple-element.74), channel_id=1, source_target_pairs={{0,16},{16,32},{32,48},{48,0},{1,17},{17,33},{33,49},{49,1},{2,18}... | collective-permute-start | bytes 221192 | tf_op jit(solution)/shard_map/ppermute | solution.py:127
  56.2 22.5 %collective-permute-start.5 = (bf16[4,2,48,384]{3,2,1,0:T(8,128)(2,1)S(1)}, bf16[4,2,48,384]{3,2,1,0:T(8,128)(2,1)S(1)}, u32[]{:S(2)}, u32[]{:S(2)}) collective-permute-start(bf16[4,2,48,384]{3,2,1,0:T(8,128)(2,1)S(1)} %pad_maximum_fusion.refs_0_), channel_id=1, source_target_pairs={{0,4},{4,8},{8,12},{12,0},{1,5},{5,9},{9,13},{13,1},{2,6},{6,10},{... | collective-permute-start | bytes 884744 | tf_op jit(solution)/shard_map/ppermute | solution.py:127
  57.7 6.2 %collective-permute-start.10 = (bf16[2,48,384]{2,1,0:T(8,128)(2,1)S(1)}, bf16[2,48,384]{2,1,0:T(8,128)(2,1)S(1)}, u32[]{:S(2)}, u32[]{:S(2)}) collective-permute-start(bf16[2,48,384]{2,1,0:T(8,128)(2,1)S(1)} %get-tuple-element.73), channel_id=1, source_target_pairs={{0,12},{4,0},{8,4},{12,8},{1,13},{5,1},{9,5},{13,9},{2,14},{6,2},{... | collective-permute-start | bytes 221192 | tf_op jit(solution)/shard_map/ppermute | solution.py:127
  59.5 9.7 %collective-permute-start.9 = (bf16[2,48,384]{2,1,0:T(8,128)(2,1)S(1)}, bf16[2,48,384]{2,1,0:T(8,128)(2,1)S(1)}, u32[]{:S(2)}, u32[]{:S(2)}) collective-permute-start(bf16[2,48,384]{2,1,0:T(8,128)(2,1)S(1)} %get-tuple-element.73), channel_id=1, source_target_pairs={{0,8},{4,12},{8,0},{12,4},{1,9},{5,13},{9,1},{13,5},{2,10},{6,14},... | collective-permute-start | bytes 221192 | tf_op jit(solution)/shard_map/ppermute | solution.py:127
  60.6 9.6 %collective-permute-start.8 = (bf16[2,48,384]{2,1,0:T(8,128)(2,1)S(1)}, bf16[2,48,384]{2,1,0:T(8,128)(2,1)S(1)}, u32[]{:S(2)}, u32[]{:S(2)}) collective-permute-start(bf16[2,48,384]{2,1,0:T(8,128)(2,1)S(1)} %get-tuple-element.73), channel_id=1, source_target_pairs={{0,4},{4,8},{8,12},{12,0},{1,5},{5,9},{9,13},{13,1},{2,6},{6,10},{... | collective-permute-start | bytes 221192 | tf_op jit(solution)/shard_map/ppermute | solution.py:127
  61.1 20.4 %collective-permute-start.6 = (bf16[4,2,48,384]{3,2,1,0:T(8,128)(2,1)S(1)}, bf16[4,2,48,384]{3,2,1,0:T(8,128)(2,1)S(1)}, u32[]{:S(2)}, u32[]{:S(2)}) collective-permute-start(bf16[4,2,48,384]{3,2,1,0:T(8,128)(2,1)S(1)} %pad_maximum_fusion.refs_0_), channel_id=1, source_target_pairs={{0,8},{4,12},{8,0},{12,4},{1,9},{5,13},{9,1},{13,5},{2,10},{6,14},... | collective-permute-start | bytes 884744 | tf_op jit(solution)/shard_map/ppermute | solution.py:127
  63.9 17.6 %collective-permute-start.7 = (bf16[4,2,48,384]{3,2,1,0:T(8,128)(2,1)S(1)}, bf16[4,2,48,384]{3,2,1,0:T(8,128)(2,1)S(1)}, u32[]{:S(2)}, u32[]{:S(2)}) collective-permute-start(bf16[4,2,48,384]{3,2,1,0:T(8,128)(2,1)S(1)} %pad_maximum_fusion.refs_0_), channel_id=1, source_target_pairs={{0,12},{4,0},{8,4},{12,8},{1,13},{5,1},{9,5},{13,9},{2,14},{6,2},{... | collective-permute-start | bytes 884744 | tf_op jit(solution)/shard_map/ppermute | solution.py:127
  70.3 12.6 %collective-permute-start.11 = (bf16[4,2,48,384]{3,2,1,0:T(8,128)(2,1)S(1)}, bf16[4,2,48,384]{3,2,1,0:T(8,128)(2,1)S(1)}, u32[]{:S(2)}, u32[]{:S(2)}) collective-permute-start(bf16[4,2,48,384]{3,2,1,0:T(8,128)(2,1)S(1)} %pad_maximum_fusion.1.refs_4_), channel_id=1, source_target_pairs={{0,16},{16,32},{32,48},{48,0},{1,17},{17,33},{33,49},{49,1},{2,18}... | collective-permute-start | bytes 884744 | tf_op jit(solution)/shard_map/ppermute | solution.py:127
  78.7 8.3 %collective-permute-start.12 = (bf16[4,2,48,384]{3,2,1,0:T(8,128)(2,1)S(1)}, bf16[4,2,48,384]{3,2,1,0:T(8,128)(2,1)}, u32[]{:S(2)}, u32[]{:S(2)}) collective-permute-start(bf16[4,2,48,384]{3,2,1,0:T(8,128)(2,1)S(1)} %pad_maximum_fusion.1.refs_4_), channel_id=1, source_target_pairs={{0,32},{16,48},{32,0},{48,16},{1,33},{17,49},{33,1},{49,17},{2,34}... | collective-permute-start | bytes 884744 | tf_op jit(solution)/shard_map/ppermute | solution.py:127
  78.7 8.3 %collective-permute-start.13 = (bf16[4,2,48,384]{3,2,1,0:T(8,128)(2,1)S(1)}, bf16[4,2,48,384]{3,2,1,0:T(8,128)(2,1)}, u32[]{:S(2)}, u32[]{:S(2)}) collective-permute-start(bf16[4,2,48,384]{3,2,1,0:T(8,128)(2,1)S(1)} %pad_maximum_fusion.1.refs_4_), channel_id=1, source_target_pairs={{0,48},{16,0},{32,16},{48,32},{1,49},{17,1},{33,17},{49,33},{2,50}... | collective-permute-start | bytes 884744 | tf_op jit(solution)/shard_map/ppermute | solution.py:127
  81.4 55.2 %collective-permute-start.28 = (bf16[2,16,48,768]{3,2,0,1:T(8,128)(2,1)}, bf16[2,16,48,768]{3,2,0,1:T(8,128)(2,1)}, u32[]{:S(2)}, u32[]{:S(2)}) collective-permute-start(bf16[2,16,48,768]{3,2,0,1:T(8,128)(2,1)} %bitcast.19), channel_id=1, source_target_pairs={{0,2},{2,0},{1,3},{3,1},{4,6},{6,4},{5,7},{7,5},{8,10},{10,8},{9,1... | collective-permute-start | bytes 7077896 | tf_op jit(solution)/shard_map/ppermute | solution.py:99
  81.6 7.9 %collective-permute-start.14 = (bf16[4,2,48,384]{3,2,1,0:T(8,128)(2,1)S(1)}, bf16[4,2,48,384]{3,2,1,0:T(8,128)(2,1)}, u32[]{:S(2)}, u32[]{:S(2)}) collective-permute-start(bf16[4,2,48,384]{3,2,1,0:T(8,128)(2,1)S(1)} %pad_maximum_fusion.refs_0_), channel_id=1, source_target_pairs={{0,2},{2,0},{1,3},{3,1},{4,6},{6,4},{5,7},{7,5},{8,10},{10,8},{9,1... | collective-permute-start | bytes 884744 | tf_op jit(solution)/shard_map/ppermute | solution.py:99
  82.9 6.5 %collective-permute-start.18 = (bf16[4,2,48,384]{3,2,1,0:T(8,128)(2,1)S(1)}, bf16[4,2,48,384]{3,2,1,0:T(8,128)(2,1)}, u32[]{:S(2)}, u32[]{:S(2)}) collective-permute-start(bf16[4,2,48,384]{3,2,1,0:T(8,128)(2,1)S(1)} %pad_maximum_fusion.1.refs_4_), channel_id=1, source_target_pairs={{0,2},{2,0},{1,3},{3,1},{4,6},{6,4},{5,7},{7,5},{8,10},{10,8},{9,1... | collective-permute-start | bytes 884744 | tf_op jit(solution)/shard_map/ppermute | solution.py:99
  87.0 2.9 collective-permute-start.15
  87.0 3.0 collective-permute-start.16
  89.4 7.9 %collective-permute-start.17 = (bf16[4,2,48,384]{3,2,1,0:T(8,128)(2,1)S(1)}, bf16[4,2,48,384]{3,2,1,0:T(8,128)(2,1)S(1)}, u32[]{:S(2)}, u32[]{:S(2)}) collective-permute-start(bf16[4,2,48,384]{3,2,1,0:T(8,128)(2,1)S(1)} %collective-permute-done.7.refs_3_), channel_id=1, source_target_pairs={{0,2},{2,0},{1,3},{3,1},{4,6},{6,4},{5,7},{7,5},{8,10},{10,8},{9,1... | collective-permute-start | bytes 884744 | tf_op jit(solution)/shard_map/ppermute | solution.py:99
  89.4 7.9 %collective-permute-start.19 = (bf16[4,2,48,384]{3,2,1,0:T(8,128)(2,1)S(1)}, bf16[4,2,48,384]{3,2,1,0:T(8,128)(2,1)S(1)}, u32[]{:S(2)}, u32[]{:S(2)}) collective-permute-start(bf16[4,2,48,384]{3,2,1,0:T(8,128)(2,1)S(1)} %collective-permute-done.11.refs_5_), channel_id=1, source_target_pairs={{0,2},{2,0},{1,3},{3,1},{4,6},{6,4},{5,7},{7,5},{8,10},{10,8},{9,1... | collective-permute-start | bytes 884744 | tf_op jit(solution)/shard_map/ppermute | solution.py:99
  89.9 7.4 %collective-permute-start.20 = (bf16[4,2,48,384]{3,2,1,0:T(8,128)(2,1)}, bf16[4,2,48,384]{3,2,1,0:T(8,128)(2,1)S(1)}, u32[]{:S(2)}, u32[]{:S(2)}) collective-permute-start(bf16[4,2,48,384]{3,2,1,0:T(8,128)(2,1)} %collective-permute-done.12.refs_6_), channel_id=1, source_target_pairs={{0,2},{2,0},{1,3},{3,1},{4,6},{6,4},{5,7},{7,5},{8,10},{10,8},{9,1... | collective-permute-start | bytes 884744 | tf_op jit(solution)/shard_map/ppermute | solution.py:99
  90.0 7.3 %collective-permute-start.21 = (bf16[4,2,48,384]{3,2,1,0:T(8,128)(2,1)}, bf16[4,2,48,384]{3,2,1,0:T(8,128)(2,1)S(1)}, u32[]{:S(2)}, u32[]{:S(2)}) collective-permute-start(bf16[4,2,48,384]{3,2,1,0:T(8,128)(2,1)} %collective-permute-done.13.refs_7_), channel_id=1, source_target_pairs={{0,2},{2,0},{1,3},{3,1},{4,6},{6,4},{5,7},{7,5},{8,10},{10,8},{9,1... | collective-permute-start | bytes 884744 | tf_op jit(solution)/shard_map/ppermute | solution.py:99
  105.4 21.9 %collective-permute-start.22 = (bf16[512,768]{1,0:T(8,128)(2,1)}, bf16[512,768]{1,0:T(8,128)(2,1)S(1)}, u32[]{:S(2)}, u32[]{:S(2)}) collective-permute-start(bf16[512,768]{1,0:T(8,128)(2,1)} %get-tuple-element.28), channel_id=1, source_target_pairs={{0,1},{1,0},{2,3},{3,2},{4,5},{5,4},{6,7},{7,6},{8,9},{9,8},{10,11... | collective-permute-start | bytes 2359304 | tf_op jit(solution)/shard_map/ppermute | solution.py:99
  112.2 14.9 %collective-permute-start.23 = (f32[2,768]{1,0:T(2,128)S(1)}, f32[2,768]{1,0:T(2,128)S(1)}, u32[]{:S(2)}, u32[]{:S(2)}) collective-permute-start(f32[2,768]{1,0:T(2,128)S(1)} %add.156), channel_id=1, source_target_pairs={{0,1},{1,0},{2,3},{3,2},{4,5},{5,4},{6,7},{7,6},{8,9},{9,8},{10,11... | collective-permute-start | bytes 18440 | tf_op jit(solution)/shard_map/ppermute | solution.py:99
  134.5 20.4 %collective-permute-start.29 = (bf16[512,768]{1,0:T(8,128)(2,1)}, bf16[512,768]{1,0:T(8,128)(2,1)S(1)}, u32[]{:S(2)}, u32[]{:S(2)}) collective-permute-start(bf16[512,768]{1,0:T(8,128)(2,1)} %get-tuple-element.31.refs_0_), channel_id=1, source_target_pairs={{0,1},{1,0},{2,3},{3,2},{4,5},{5,4},{6,7},{7,6},{8,9},{9,8},{10,11... | collective-permute-start | bytes 2359304 | tf_op jit(solution)/shard_map/ppermute | solution.py:99
  159.9 5.3 %collective-permute-start.30 = (f32[6,512]{1,0:T(8,128)S(1)}, f32[6,512]{1,0:T(8,128)S(1)}, u32[]{:S(2)}, u32[]{:S(2)}) collective-permute-start(f32[6,512]{1,0:T(8,128)S(1)} %stack.115), channel_id=1, source_target_pairs={{0,1},{1,0},{2,3},{3,2},{4,5},{5,4},{6,7},{7,6},{8,9},{9,8},{10,11... | collective-permute-start | bytes 36872 | tf_op jit(solution)/shard_map/ppermute | solution.py:99
  162.1 8.8 %collective-permute-start.35 = (bf16[512,768]{1,0:T(8,128)(2,1)}, bf16[512,768]{1,0:T(8,128)(2,1)}, u32[]{:S(2)}, u32[]{:S(2)}) collective-permute-start(bf16[512,768]{1,0:T(8,128)(2,1)} %get-tuple-element.31.refs_0_), channel_id=1, source_target_pairs={{0,2},{2,0},{1,3},{3,1},{4,6},{6,4},{5,7},{7,5},{8,10},{10,8},{9,1... | collective-permute-start | bytes 2359304 | tf_op jit(solution)/shard_map/ppermute | solution.py:99
  162.1 8.8 %collective-permute-start.36 = (bf16[512,768]{1,0:T(8,128)(2,1)}, bf16[512,768]{1,0:T(8,128)(2,1)}, u32[]{:S(2)}, u32[]{:S(2)}) collective-permute-start(bf16[512,768]{1,0:T(8,128)(2,1)} %copy-done.30), channel_id=1, source_target_pairs={{0,2},{2,0},{1,3},{3,1},{4,6},{6,4},{5,7},{7,5},{8,10},{10,8},{9,1... | collective-permute-start | bytes 2359304 | tf_op jit(solution)/shard_map/ppermute | solution.py:99
  179.3 64.4 %all-to-all-start.1 = ((bf16[16,2,48,768]{3,2,1,0:T(8,128)(2,1)}), bf16[16,2,48,768]{3,2,1,0:T(8,128)(2,1)}, u32[]{:S(2)}, u32[]{:S(2)}) async-start(bf16[16,2,48,768]{3,2,1,0:T(8,128)(2,1)} %shard_map.123), calls=%async_computation.1 | async-start | bytes 4718592 | tf_op jit(solution)/shard_map/all_to_all | solution.py:219
  188.5 21.2 %collective-permute-start.31 = (bf16[512,768]{1,0:T(8,128)(2,1)S(1)}, bf16[512,768]{1,0:T(8,128)(2,1)}, u32[]{:S(2)}, u32[]{:S(2)}) collective-permute-start(bf16[512,768]{1,0:T(8,128)(2,1)S(1)} %convolution_convert_fusion), channel_id=1, source_target_pairs={{0,1},{1,0},{2,3},{3,2},{4,5},{5,4},{6,7},{7,6},{8,9},{9,8},{10,11... | collective-permute-start | bytes 2359304 | tf_op jit(solution)/shard_map/ppermute | solution.py:99
  219.3 20.2 %collective-permute-start.32 = (bf16[512,768]{1,0:T(8,128)(2,1)}, bf16[512,768]{1,0:T(8,128)(2,1)}, u32[]{:S(2)}, u32[]{:S(2)}) collective-permute-start(bf16[512,768]{1,0:T(8,128)(2,1)} %get-tuple-element.33.refs_0_), channel_id=1, source_target_pairs={{0,1},{1,0},{2,3},{3,2},{4,5},{5,4},{6,7},{7,6},{8,9},{9,8},{10,11... | collective-permute-start | bytes 2359304 | tf_op jit(solution)/shard_map/ppermute | solution.py:99
  221.4 18.1 %collective-permute-start.34 = (bf16[512,768]{1,0:T(8,128)(2,1)}, bf16[512,768]{1,0:T(8,128)(2,1)}, u32[]{:S(2)}, u32[]{:S(2)}) collective-permute-start(bf16[512,768]{1,0:T(8,128)(2,1)} %get-tuple-element.25.refs_17_), channel_id=1, source_target_pairs={{0,2},{2,0},{1,3},{3,1},{4,6},{6,4},{5,7},{7,5},{8,10},{10,8},{9,1... | collective-permute-start | bytes 2359304 | tf_op jit(solution)/shard_map/ppermute | solution.py:99
  221.4 18.1 %collective-permute-start.33 = (bf16[512,768]{1,0:T(8,128)(2,1)}, bf16[512,768]{1,0:T(8,128)(2,1)}, u32[]{:S(2)}, u32[]{:S(2)}) collective-permute-start(bf16[512,768]{1,0:T(8,128)(2,1)} %get-tuple-element.33.refs_0_), channel_id=1, source_target_pairs={{0,2},{2,0},{1,3},{3,1},{4,6},{6,4},{5,7},{7,5},{8,10},{10,8},{9,1... | collective-permute-start | bytes 2359304 | tf_op jit(solution)/shard_map/ppermute | solution.py:99
  239.5 19.0 %collective-permute-start.38 = (bf16[512,768]{1,0:T(8,128)(2,1)}, bf16[512,768]{1,0:T(8,128)(2,1)}, u32[]{:S(2)}, u32[]{:S(2)}) collective-permute-start(bf16[512,768]{1,0:T(8,128)(2,1)} %collective-permute-done.32.refs_0_), channel_id=1, source_target_pairs={{0,2},{2,0},{1,3},{3,1},{4,6},{6,4},{5,7},{7,5},{8,10},{10,8},{9,1... | collective-permute-start | bytes 2359304 | tf_op jit(solution)/shard_map/ppermute | solution.py:99
  243.6 26.8 %all-to-all-start.2 = ((bf16[16,1,48,768]{3,2,1,0:T(8,128)(2,1)}), bf16[16,1,48,768]{3,2,1,0:T(8,128)(2,1)}, u32[]{:S(2)}, u32[]{:S(2)}) async-start(bf16[16,1,48,768]{3,2,1,0:T(8,128)(2,1)} %shard_map.122), calls=%async_computation.2 | async-start | bytes 2359296 | tf_op jit(solution)/shard_map/all_to_all | solution.py:219
  270.4 22.6 %all-to-all-start.3 = ((bf16[16,1,48,768]{3,2,1,0:T(8,128)(2,1)}), bf16[16,1,48,768]{3,2,1,0:T(8,128)(2,1)}, u32[]{:S(2)}, u32[]{:S(2)}) async-start(bf16[16,1,48,768]{3,2,1,0:T(8,128)(2,1)} %shard_map.124), calls=%async_computation.3 | async-start | bytes 2359296 | tf_op jit(solution)/shard_map/all_to_all | solution.py:219
  275.7 7.3 %collective-permute-start.43 = (f32[24,768]{1,0:T(8,128)S(1)}, f32[24,768]{1,0:T(8,128)S(1)}, u32[]{:S(2)}, u32[]{:S(2)}) collective-permute-start(f32[24,768]{1,0:T(8,128)S(1)} %get-tuple-element.64), channel_id=1, source_target_pairs={{0,64},{64,0},{1,65},{65,1},{2,66},{66,2},{3,67},{67,3},{4,68},{68... | collective-permute-start | bytes 221192 | tf_op jit(solution)/shard_map/ppermute | solution.py:99
  275.9 7.1 %collective-permute-start.44 = (f32[24,768]{1,0:T(8,128)S(1)}, f32[24,768]{1,0:T(8,128)S(1)}, u32[]{:S(2)}, u32[]{:S(2)}) collective-permute-start(f32[24,768]{1,0:T(8,128)S(1)} %get-tuple-element.63), channel_id=1, source_target_pairs={{0,66},{2,64},{64,2},{66,0},{1,67},{3,65},{65,3},{67,1},{4,70},{6,... | collective-permute-start | bytes 221192 | tf_op jit(solution)/shard_map/ppermute | solution.py:233
  275.9 7.1 %collective-permute-start.45 = (f32[24,768]{1,0:T(8,128)S(1)}, f32[24,768]{1,0:T(8,128)S(1)}, u32[]{:S(2)}, u32[]{:S(2)}) collective-permute-start(f32[24,768]{1,0:T(8,128)S(1)} %select_bitcast_fusion), channel_id=1, source_target_pairs={{0,2},{2,0},{1,3},{3,1},{4,6},{6,4},{5,7},{7,5},{8,10},{10,8},{9,1... | collective-permute-start | bytes 221192 | tf_op jit(solution)/shard_map/ppermute | solution.py:99
  295.5 4.4 %collective-permute-start.39 = (f32[24,768]{1,0:T(8,128)S(1)}, f32[24,768]{1,0:T(8,128)S(1)}, u32[]{:S(2)}, u32[]{:S(2)}) collective-permute-start(f32[24,768]{1,0:T(8,128)S(1)} %get-tuple-element.68), channel_id=1, source_target_pairs={{0,64},{64,0},{1,65},{65,1},{2,66},{66,2},{3,67},{67,3},{4,68},{68... | collective-permute-start | bytes 221192 | tf_op jit(solution)/shard_map/ppermute | solution.py:99
  295.8 9.5 %collective-permute-start.46 = (f32[24]{0:T(128)S(1)}, f32[24]{0:T(128)S(1)}, u32[]{:S(2)}, u32[]{:S(2)}) collective-permute-start(f32[24]{0:T(128)S(1)} %multiply_reduce_fusion.3), channel_id=1, source_target_pairs={{0,1},{1,0},{2,3},{3,2},{4,5},{5,4},{6,7},{7,6},{8,9},{9,8},{10,11... | collective-permute-start | bytes 296 | tf_op jit(solution)/shard_map/ppermute | solution.py:99
  299.4 6.0 %collective-permute-start.40 = (f32[24,768]{1,0:T(8,128)S(1)}, f32[24,768]{1,0:T(8,128)S(1)}, u32[]{:S(2)}, u32[]{:S(2)}) collective-permute-start(f32[24,768]{1,0:T(8,128)S(1)} %get-tuple-element.67), channel_id=1, source_target_pairs={{0,66},{2,64},{64,2},{66,0},{1,67},{3,65},{65,3},{67,1},{4,70},{6,... | collective-permute-start | bytes 221192 | tf_op jit(solution)/shard_map/ppermute | solution.py:233
  300.0 5.4 %collective-permute-start.41 = (f32[24,768]{1,0:T(8,128)S(1)}, f32[24,768]{1,0:T(8,128)S(1)}, u32[]{:S(2)}, u32[]{:S(2)}) collective-permute-start(f32[24,768]{1,0:T(8,128)S(1)} %get-tuple-element.65), channel_id=1, source_target_pairs={{0,2},{2,0},{1,3},{3,1},{4,6},{6,4},{5,7},{7,5},{8,10},{10,8},{9,1... | collective-permute-start | bytes 221192 | tf_op jit(solution)/shard_map/ppermute | solution.py:99
  305.6 5.1 %collective-permute-start.42 = (f32[24]{0:T(128)S(1)}, f32[24]{0:T(128)S(1)}, u32[]{:S(2)}, u32[]{:S(2)}) collective-permute-start(f32[24]{0:T(128)S(1)} %multiply_reduce_fusion.4), channel_id=1, source_target_pairs={{0,1},{1,0},{2,3},{3,2},{4,5},{5,4},{6,7},{7,6},{8,9},{9,8},{10,11... | collective-permute-start | bytes 296 | tf_op jit(solution)/shard_map/ppermute | solution.py:99
  (35 other events, 330.9 us)
